TPU v7x, 32 devices: a whole 2x2x4 slice. The times are simulated.
32 devices in a mesh: groups: 2 (over x), tm: 4 (over y, core), rows: 4 (over z).
Axes of the slice: x: 2, y: 2, z: 4, core: 2. Of those that a mesh axis runs over, the one named last changes fastest.
Arguments:
- features: bfloat16 [16, 8, 96, 512], P(('groups', 'tm'), 'rows'), parts along dimension 0, may hold values from -6 to 6
- spatial_weight: bfloat16 [3, 3, 512, 512], replicated, may hold values from -0.09375 to 0.09375
- temporal_weight: bfloat16 [3, 512, 512], replicated, may hold values from -0.15625 to 0.15625
- head_weight: bfloat16 [512, 16], replicated, may hold values from -0.25 to 0.25
- embed_weight: bfloat16 [64, 5120], replicated, may hold values from -0.75 to 0.75
- ada_scale: bfloat16 [5120], replicated, may hold values from -0.5 to 0.5
- ada_shift: bfloat16 [5120], replicated, may hold values from -3 to 3
- qkv_weight: bfloat16 [5120, 9216], P('tm', 'rows'), may hold values from -0.078125 to 0.078125
Outputs:
- qkv: float32 [3072, 9216], P(('groups', 'tm'), 'rows'), parts along dimension 0
There are 2 independent parts, one for each index of `groups`. A program takes and returns all parts, laid end to end along the dimension named above; an argument that names none is the same for every part. Nothing has to cross between parts.
All inputs are finite; a program needn't handle non-finite values.
Results may differ from a plain program's by a relative error of at most 0.0056.
Values may be sent and summed in bfloat16 or wider, within the bound.
A program may use at most 128 MiB of HBM per device.

v0:
```python
import jax
import jax.numpy as jnp
from jax import lax
from jax.sharding import PartitionSpec as P

LATENT = 16
PATCH = 2
PDIM = 64


def with_halo(cells, sides, width):
    for axis, dim in sides:
        count = lax.axis_size(axis)
        ends = count - 1
        head = lax.slice_in_dim(cells, 0, width, axis=dim)
        tail = lax.slice_in_dim(cells, cells.shape[dim] - width, cells.shape[dim], axis=dim)
        cells = jnp.concatenate(
            [
                lax.ppermute(tail, axis, [(i, (i + 1) % count) for i in range(ends)]),
                cells,
                lax.ppermute(head, axis, [((i + 1) % count, i) for i in range(ends)]),
            ],
            axis=dim,
        )
    return cells


def passed_along(block, axis, distance):
    devices = range(lax.axis_size(axis))
    route = [(i - distance, i) for i in devices if i - distance in devices]
    return lax.ppermute(block, axis, route)


def halves(values):
    high = lax.reduce_precision(values, 8, 7)
    return high.astype(jnp.bfloat16), (values - high).astype(jnp.bfloat16)


def summed_over(values, axis):
    count = lax.axis_size(axis)
    if count & (count - 1):
        return lax.psum(values, axis)
    step = 1
    while step < count:
        values = values + lax.ppermute(values, axis, [(i, i ^ step) for i in range(count)])
        step *= 2
    return values


def norm_silu(values):
    scaled = values * lax.rsqrt(jnp.mean(values * values, axis=-1, keepdims=True) + 1e-06)
    return jax.nn.silu(scaled)


def per_device(
    features,
    spatial_weight,
    temporal_weight,
    head_weight,
    embed_weight,
    ada_scale,
    ada_shift,
    qkv_weight,
):
    frames_dev, rows_dev, columns, channels = features.shape
    depth = qkv_weight.shape[0]
    start = lax.axis_index("tm") * depth
    wide = embed_weight.astype(jnp.float32)
    wide = wide - jnp.mean(wide, axis=1, keepdims=True)
    gram = lax.dot_general(
        wide, wide, (((1,), (1,)), ((), ())), precision=lax.Precision.HIGHEST
    ) / wide.shape[1]
    scaled = lax.dynamic_slice_in_dim(
        wide * (1.0 + ada_scale.astype(jnp.float32)), start, depth, axis=1
    )
    shift = lax.dynamic_slice_in_dim(ada_shift, start, depth, axis=0)
    terms = jnp.dot(
        jnp.concatenate([*halves(scaled), shift[None]], axis=0),
        qkv_weight,
        preferred_element_type=jnp.float32,
    )
    folded = summed_over(
        jnp.concatenate([terms[:PDIM] + terms[PDIM : 2 * PDIM], terms[2 * PDIM :]], axis=0), "tm"
    )
    activated = norm_silu(features.astype(jnp.float32)).astype(jnp.bfloat16)
    rimmed = with_halo(activated, (("rows", 1),), 1)
    padded = jnp.pad(rimmed, ((0, 0), (0, 0), (1, 1), (0, 0)))
    spatial = jnp.zeros((frames_dev * rows_dev * columns, channels), jnp.float32)
    for tap_row in range(3):
        for tap_col in range(3):
            window = padded[:, tap_row : tap_row + rows_dev, tap_col : tap_col + columns].reshape(
                -1, channels
            )
            spatial = spatial + jnp.dot(
                window, spatial_weight[tap_row, tap_col], preferred_element_type=jnp.float32
            )
    mixed_act = (
        norm_silu(spatial).astype(jnp.bfloat16).reshape(frames_dev, rows_dev, columns, channels)
    )
    before = passed_along(mixed_act, "tm", 1)
    stacked = jnp.concatenate([before, mixed_act], axis=0)
    temporal = jnp.zeros((frames_dev * rows_dev * columns, channels), jnp.float32)
    for tap in range(3):
        temporal = temporal + jnp.dot(
            stacked[tap : tap + frames_dev].reshape(-1, channels),
            temporal_weight[tap],
            preferred_element_type=jnp.float32,
        )
    summed = features.astype(jnp.float32).reshape(-1, channels) + temporal
    latent = jnp.dot(
        norm_silu(summed).astype(jnp.bfloat16), head_weight, preferred_element_type=jnp.float32
    ).astype(jnp.bfloat16)
    latent = latent.reshape(frames_dev, 1, PATCH, columns // PATCH, PATCH, LATENT)
    patches = jnp.transpose(latent, (0, 1, 3, 2, 4, 5)).reshape(
        frames_dev, 1, columns // PATCH, PDIM
    )
    token_block = lax.all_gather(patches, "rows", axis=1, tiled=True)
    block_rows = token_block.shape[0] * token_block.shape[1] * token_block.shape[2]
    block = token_block.reshape(block_rows, PDIM)
    moment = jnp.dot(
        block.astype(jnp.float32), gram, precision=lax.Precision.HIGHEST
    ) * block.astype(jnp.float32)
    spread = jnp.maximum(jnp.sum(moment, axis=-1, keepdims=True), 0.0)
    product = jnp.dot(
        jnp.concatenate([block, block], axis=1),
        jnp.concatenate(halves(folded[:PDIM]), axis=0),
        preferred_element_type=jnp.float32,
    )
    projected = product * lax.rsqrt(spread + 1e-06) + folded[PDIM : PDIM + 1]
    return projected


def solution(mesh):
    return jax.shard_map(
        per_device,
        mesh=mesh,
        in_specs=(
            P(("groups", "tm"), "rows", None, None),
            P(),
            P(),
            P(),
            P(),
            P(),
            P(),
            P("tm", "rows"),
        ),
        out_specs=P(("groups", "tm"), "rows"),
        check_vma=False,
    )
```

profile of v0, /device:TPU:0, one launch (start us, length us, event | category | flops | bytes accessed | tf_op | source)
XLA Modules:
  0.0 49.5 jit_solution(3732415757868189775)
XLA Ops:
  0.0 0.0 copy-start
  0.0 0.0 copy-start.2
  0.0 0.0 copy-start.4
  0.0 1.2 %multiply_reduce_fusion.2 = f32[2,2,96]{2,1,0:T(2,128)S(1)} fusion(bf16[2,2,96,512]{3,2,1,0:T(8,128)(2,1)} %param.8), kind=kLoop, calls=%fused_computation.34 | loop fusion | flops 589440 | bytes 394752 | tf_op jit(solution)/shard_map/reduce_sum | solution.py:51
  1.2 1.3 %multiply_convert_fusion.2 = bf16[2,2,96,512]{3,2,1,0:T(8,128)(2,1)S(1)} fusion(f32[2,2,96]{2,1,0:T(2,128)S(1)} %add_rsqrt_fusion.3, bf16[2,2,96,512]{3,2,1,0:T(8,128)(2,1)} %param.8), kind=kLoop, calls=%fused_computation.33 | loop fusion | flops 1376256 | bytes 787968 | tf_op jit(solution)/shard_map/convert_element_type | solution.py:85
  2.6 5.0 %collective-permute-start = (bf16[2,1,96,512]{3,2,1,0:T(8,128)(2,1)S(1)}, bf16[2,1,96,512]{3,2,1,0:T(8,128)(2,1)S(1)}, u32[]{:S(2)}, u32[]{:S(2)}) collective-permute-start(bf16[2,1,96,512]{3,2,1,0:T(8,128)(2,1)S(1)} %get-tuple-element.17), channel_id=1, source_target_pairs={{0,1},{1,2},{2,3},{4,5},{5,6},{6,7},{8,9},{9,10},{10,11},{12,13},{... | collective-permute-start | bytes 589832 | tf_op jit(solution)/shard_map/ppermute | solution.py:19
  7.5 1.3 %collective-permute-start.1 = (bf16[2,1,96,512]{3,2,1,0:T(8,128)(2,1)S(1)}, bf16[2,1,96,512]{3,2,1,0:T(8,128)(2,1)S(1)}, u32[]{:S(2)}, u32[]{:S(2)}) collective-permute-start(bf16[2,1,96,512]{3,2,1,0:T(8,128)(2,1)S(1)} %get-tuple-element.18), channel_id=1, source_target_pairs={{1,0},{2,1},{3,2},{5,4},{6,5},{7,6},{9,8},{10,9},{11,10},{13,12},{... | collective-permute-start | bytes 589832 | tf_op jit(solution)/shard_map/ppermute | solution.py:21
  8.8 0.0 copy-done.2
  8.9 0.2 convert_reduce_fusion
  9.1 0.0 copy-done.4
  9.1 0.2 convert_subtract_fusion
  9.3 0.1 dynamic-slice
  9.3 0.8 %dynamic_slice.7 = bf16[1280]{0:T(1024)(128)(2,1)S(1)} dynamic-slice(bf16[5120]{0:T(1024)(128)(2,1)} %param.14, s32[]{:T(128)S(6)} %select_n.4), dynamic_slice_sizes={1280} | dynamic-slice | bytes 5124 | tf_op jit(solution)/shard_map/dynamic_slice | solution.py:76
  10.1 0.0 slice-start
  10.1 0.1 reduce-precision_convert_fusion.1
  10.2 0.0 slice-start.1
  10.2 3.8 %fusion.42 = f32[129,2304]{1,0:T(8,128)S(1)} fusion(bf16[1280,2304]{1,0:T(8,128)(2,1)} %param.15, bf16[1,1280]{1,0:T(2,128)(2,1)S(1)} %broadcast_in_dim.2, bf16[64,1280]{1,0:T(8,128)(2,1)S(1)} %get-tuple-element.6, bf16[64,1280]{1,0:T(8,128)(2,1)S(1)} %get-tuple-element.5), kind=kOutput, calls=%fused_computation.74 | convolution fusion | flops 761863680 | bytes 7417344 | tf_op jit(solution)/shard_map/dot_general | solution.py:77
  14.0 0.1 slice_add_fusion
  14.2 0.1 collective-permute-start.3
  14.2 0.0 collective-permute-done
  14.2 1.6 %collective-permute-done.1 = bf16[2,1,96,512]{3,2,1,0:T(8,128)(2,1)S(1)} collective-permute-done((bf16[2,1,96,512]{3,2,1,0:T(8,128)(2,1)S(1)}, bf16[2,1,96,512]{3,2,1,0:T(8,128)(2,1)S(1)}, u32[]{:S(2)}, u32[]{:S(2)}) %collective-permute-start.1) | collective-permute-done | bytes 196640 | tf_op jit(solution)/shard_map/ppermute | solution.py:21
  15.8 0.2 fusion.9
  16.0 0.3 fusion.56
  16.4 0.0 slice-done
  16.4 0.0 slice-done.1
  16.4 0.4 fusion.28
  16.8 0.4 fusion.19
  17.1 0.1 pad_maximum_fusion.2
  17.2 0.4 convolution_add_fusion.7
  17.6 0.4 convolution_add_fusion.6
  17.9 0.4 convolution_add_fusion.5
  18.3 0.4 convolution_add_fusion.4
  18.7 0.4 convolution_add_fusion.3
  19.1 0.4 convolution_add_fusion.2
  19.4 0.5 multiply_reduce_fusion.1
  19.9 0.0 copy-start.3
  19.9 0.3 multiply_convert_fusion.1
  20.2 1.4 %collective-permute-start.2 = (bf16[2,2,96,512]{3,2,1,0:T(8,128)(2,1)S(1)}, bf16[2,2,96,512]{3,2,1,0:T(8,128)(2,1)S(1)}, u32[]{:S(2)}, u32[]{:S(2)}) collective-permute-start(bf16[2,2,96,512]{3,2,1,0:T(8,128)(2,1)S(1)} %bitcast.80), channel_id=1, source_target_pairs={{0,4},{4,8},{8,12},{1,5},{5,9},{9,13},{2,6},{6,10},{10,14},{3,7},{... | collective-permute-start | bytes 1179656 | tf_op jit(solution)/shard_map/ppermute | solution.py:31
  21.7 1.4 %convolution_multiply_fusion.2 = f32[64,64]{1,0:T(8,128)S(1)} fusion(bf16[64,5120]{1,0:T(8,128)(2,1)S(1)} %copy-done.2, f32[64]{0:T(128)S(1)} %broadcast_multiply_fusion), kind=kOutput, calls=%fused_computation.20 | convolution fusion | flops 252317696 | bytes 672000 | tf_op jit(solution)/shard_map/dot_general | solution.py:70
  23.1 0.0 copy-done.3
  23.1 0.4 fusion.14
  23.5 0.0 copy-start.1
  23.5 0.0 collective-permute-done.2
  23.5 0.4 fusion.16
  23.9 0.6 %copy-done.1 = bf16[2,2,96,512]{3,2,1,0:T(8,128)(2,1)S(1)} copy-done((bf16[2,2,96,512]{3,2,1,0:T(8,128)(2,1)S(1)}, bf16[2,2,96,512]{3,2,1,0:T(8,128)(2,1)}, u32[]{:S(2)}) %copy-start.1) | copy-done | bytes 393240
  24.5 0.5 %multiply_reduce_fusion = (f32[384]{0:T(512)S(1)}, f32[384,512]{1,0:T(8,128)S(1)}) fusion(f32[384,512]{1,0:T(8,128)S(1)} %fusion.14, f32[384,512]{1,0:T(8,128)S(1)} %fusion.16, bf16[384,512]{1,0:T(8,128)(2,1)S(1)} %bitcast.86, bf16[3,512,512]{2,1,0:T(8,128)(2,1)S(1)} %copy-done.3, bf16[384,512]{1,0:T(8,128)(2,1)S(1)} %bitcast.79), kind=kOutput, calls=%fused_computation.30 | convolution fusion | flops 202505856 | bytes 3671552 | tf_op jit(solution)/shard_map/dot_general | solution.py:104
  25.0 0.0 collective-permute-done.3
  25.0 0.1 fusion.55
  25.1 7.0 %collective-permute-start.4 = (f32[65,2304]{1,0:T(8,128)S(1)}, f32[65,2304]{1,0:T(8,128)S(1)}, u32[]{:S(2)}, u32[]{:S(2)}) collective-permute-start(f32[65,2304]{1,0:T(8,128)S(1)} %fusion.55), channel_id=1, source_target_pairs={{0,8},{4,12},{8,0},{12,4},{1,9},{5,13},{9,1},{13,5},{2,10},{6,14},... | collective-permute-start | bytes 1797128 | tf_op jit(solution)/shard_map/ppermute | solution.py:45
  32.1 0.0 copy-done
  32.1 0.4 convolution_convert_fusion
  32.5 0.2 copy.12
  32.6 0.1 copy.13
  32.7 0.1 copy.14
  32.9 13.5 %all_gather.3 = bf16[2,4,48,64]{3,2,0,1:T(8,128)(2,1)S(1)} all-gather(bf16[2,1,48,64]{3,2,0,1:T(8,128)(2,1)S(1)} %copy.14), channel_id=1, replica_groups=mesh['groups'=2,'tm'=4,'rows'=4] {'rows'}, dimensions={1}, use_global_device_ids=true | all-gather | bytes 61440 | tf_op jit(solution)/shard_map/all_gather | solution.py:117
  46.3 0.1 copy.15
  46.5 0.1 reshape.100
  46.6 0.3 fusion.4
  46.9 0.0 collective-permute-done.4
  46.9 0.1 add.133
  47.0 0.1 reduce-precision_convert_fusion
  47.1 2.5 %broadcast_add_fusion = f32[384,2304]{1,0:T(8,128)} fusion(f32[2304]{0:T(1024)S(1)} %slice_reduce_fusion, f32[384]{0:T(512)S(1)} %add_rsqrt_fusion, bf16[64,2304]{1,0:T(8,128)(2,1)S(1)} %get-tuple-element.14, bf16[64,2304]{1,0:T(8,128)(2,1)S(1)} %get-tuple-element.13, bf16[384,64]{0,1:T(8,128)(2,1)S(1)} %reshape.100), kind=kOutput, calls=%fused_computation.3 | convolution fusion | flops 229638144 | bytes 4188672 | tf_op jit(solution)/shard_map/dot_general | solution.py:124
  (13 shorter events, 0.2 us)
Async XLA Ops:
  0.0 32.1 %copy-start = (bf16[512,16]{0,1:T(8,128)(2,1)S(1)}, bf16[512,16]{0,1:T(8,128)(2,1)}, u32[]{:S(2)}) copy-start(bf16[512,16]{0,1:T(8,128)(2,1)} %param.11) | copy-start | bytes 49156
  0.0 8.8 %copy-start.2 = (bf16[64,5120]{1,0:T(8,128)(2,1)S(1)}, bf16[64,5120]{1,0:T(8,128)(2,1)}, u32[]{:S(2)}) copy-start(bf16[64,5120]{1,0:T(8,128)(2,1)} %param.12) | copy-start | bytes 1966084
  0.0 9.1 %copy-start.4 = (bf16[5120]{0:T(1024)(128)(2,1)S(1)}, bf16[5120]{0:T(1024)(128)(2,1)}, u32[]{:S(2)}) copy-start(bf16[5120]{0:T(1024)(128)(2,1)} %param.13) | copy-start | bytes 30724
  2.6 11.7 %collective-permute-start = (bf16[2,1,96,512]{3,2,1,0:T(8,128)(2,1)S(1)}, bf16[2,1,96,512]{3,2,1,0:T(8,128)(2,1)S(1)}, u32[]{:S(2)}, u32[]{:S(2)}) collective-permute-start(bf16[2,1,96,512]{3,2,1,0:T(8,128)(2,1)S(1)} %get-tuple-element.17), channel_id=1, source_target_pairs={{0,1},{1,2},{2,3},{4,5},{5,6},{6,7},{8,9},{9,10},{10,11},{12,13},{... | collective-permute-start | bytes 589832 | tf_op jit(solution)/shard_map/ppermute | solution.py:19
  7.5 8.3 %collective-permute-start.1 = (bf16[2,1,96,512]{3,2,1,0:T(8,128)(2,1)S(1)}, bf16[2,1,96,512]{3,2,1,0:T(8,128)(2,1)S(1)}, u32[]{:S(2)}, u32[]{:S(2)}) collective-permute-start(bf16[2,1,96,512]{3,2,1,0:T(8,128)(2,1)S(1)} %get-tuple-element.18), channel_id=1, source_target_pairs={{1,0},{2,1},{3,2},{5,4},{6,5},{7,6},{9,8},{10,9},{11,10},{13,12},{... | collective-permute-start | bytes 589832 | tf_op jit(solution)/shard_map/ppermute | solution.py:21
  10.1 6.2 %slice-start = ((s8[4718592]{0:T(1024)(128)(4,1)}), s8[4194304]{0:T(1024)(128)(4,1)S(1)}, s32[]{:S(2)}) async-start(s8[4718592]{0:T(1024)(128)(4,1)} %bitcast.77), calls=%async_computation | async-start | bytes 8388608
  10.2 6.2 %slice-start.1 = ((s8[4718592]{0:T(1024)(128)(4,1)}), s8[524288]{0:T(1024)(128)(4,1)S(1)}, s32[]{:S(2)}) async-start(s8[4718592]{0:T(1024)(128)(4,1)} %bitcast.77), calls=%async_computation.1 | async-start | bytes 1048576
  14.2 10.8 %collective-permute-start.3 = (f32[65,2304]{1,0:T(8,128)S(1)}, f32[65,2304]{1,0:T(8,128)S(1)}, u32[]{:S(2)}, u32[]{:S(2)}) collective-permute-start(f32[65,2304]{1,0:T(8,128)S(1)} %pad_maximum_fusion), channel_id=1, source_target_pairs={{0,4},{4,0},{8,12},{12,8},{1,5},{5,1},{9,13},{13,9},{2,6},{6,2},{1... | collective-permute-start | bytes 1797128 | tf_op jit(solution)/shard_map/ppermute | solution.py:45
  19.9 3.2 %copy-start.3 = (bf16[3,512,512]{2,1,0:T(8,128)(2,1)S(1)}, bf16[3,512,512]{2,1,0:T(8,128)(2,1)}, u32[]{:S(2)}) copy-start(bf16[3,512,512]{2,1,0:T(8,128)(2,1)} %param.10) | copy-start | bytes 4718596
  20.2 3.3 %collective-permute-start.2 = (bf16[2,2,96,512]{3,2,1,0:T(8,128)(2,1)S(1)}, bf16[2,2,96,512]{3,2,1,0:T(8,128)(2,1)S(1)}, u32[]{:S(2)}, u32[]{:S(2)}) collective-permute-start(bf16[2,2,96,512]{3,2,1,0:T(8,128)(2,1)S(1)} %bitcast.80), channel_id=1, source_target_pairs={{0,4},{4,8},{8,12},{1,5},{5,9},{9,13},{2,6},{6,10},{10,14},{3,7},{... | collective-permute-start | bytes 1179656 | tf_op jit(solution)/shard_map/ppermute | solution.py:31
  23.5 1.0 %copy-start.1 = (bf16[2,2,96,512]{3,2,1,0:T(8,128)(2,1)S(1)}, bf16[2,2,96,512]{3,2,1,0:T(8,128)(2,1)}, u32[]{:S(2)}) copy-start(bf16[2,2,96,512]{3,2,1,0:T(8,128)(2,1)} %param.8) | copy-start | bytes 1179652
  25.1 21.8 %collective-permute-start.4 = (f32[65,2304]{1,0:T(8,128)S(1)}, f32[65,2304]{1,0:T(8,128)S(1)}, u32[]{:S(2)}, u32[]{:S(2)}) collective-permute-start(f32[65,2304]{1,0:T(8,128)S(1)} %fusion.55), channel_id=1, source_target_pairs={{0,8},{4,12},{8,0},{12,4},{1,9},{5,13},{9,1},{13,5},{2,10},{6,14},... | collective-permute-start | bytes 1797128 | tf_op jit(solution)/shard_map/ppermute | solution.py:45
where the time goes:
time: 49.8 us; the launch traced here: 49.5 us
  starting transfers between devices  14.8 us (30%)
  blocking collectives  13.5 us (27%)
  matrix products  12.9 us (26%)
  other arithmetic  3.92 us (8%)
  local copies, waits for them, and re-layouts  2.46 us (5%)
  waiting for transfers between devices  1.57 us (3%)
    all_gather x1, blocking collectives, per_device(): token_block = lax.all_gather(patches, 'rows', axis=1, tiled=True)  13.5 us
    ppermute x2, starting transfers between devices, summed_over(): lax.ppermute(values, axis, [(i, i ^ step) for i in range(count)])  7.07 us
    ppermute x1, starting transfers between devices, with_halo(): lax.ppermute(tail, axis, [(i, (i + 1) % count) for i in range(ends)])  4.97 us
    dot_general x1, matrix products, per_device(): jnp.dot(jnp.concatenate([*halves(scaled), shift[None]], axis=0), qkv_weig...  3.81 us
    dot_general x9, matrix products, per_device(): jnp.dot(window, spatial_weight[tap_row, tap_col], preferred_element_type=...  3.38 us
    dot_general x1, matrix products, per_device(): jnp.dot(jnp.concatenate([block, block], axis=1), jnp.concatenate(halves(f...  2.45 us
    ppermute x1, waiting for transfers between devices, with_halo(): lax.ppermute(head, axis, [((i + 1) % count, i) for i in range(ends)])  1.56 us
    ppermute x1, starting transfers between devices, passed_along(): return lax.ppermute(block, axis, route)  1.45 us
  transfers between devices with their start and end apart: 5, of which 1 were waited for; matrix products, arithmetic and copies ran while one was open for 27% of the time, Pallas kernels for 0%

commit v1 on v0

v1 whole, which is shorter than its diff:
```python
import functools

import jax
import jax.numpy as jnp
from jax import lax
from jax.experimental import pallas as pl
from jax.experimental.pallas import tpu as pltpu
from jax.sharding import PartitionSpec as P

MESH = pl.DeviceIdType.MESH
PATCH = 2
LANES = 128
EPS = 1e-06
F32 = jnp.float32
BF16 = jnp.bfloat16


def dot(a, b):
    return jnp.dot(a, b, preferred_element_type=F32)


def dot_t(a, b):
    return lax.dot_general(a, b, (((1,), (1,)), ((), ())), preferred_element_type=F32)


def norm_silu(values):
    scaled = values * lax.rsqrt(jnp.mean(values * values, axis=-1, keepdims=True) + EPS)
    half = 0.5 * scaled
    return half + half * jnp.tanh(half)


def encode(
    n_groups, n_tm, n_rows, split, aligned,
    features, spatial_hbm, temporal_hbm, head_hbm, embed_hbm, part_ref, scale_ref, shift_ref, qkv_hbm,
    block_out, fold_out, shift_out, gram_out,
    feat, halo, taps, spat_w, temp_w, head_w, embed, wide, qkv_w, mixed, before, partial, lat,
    part_b, core_in, keep, cross, fold, shifts, shifts_in, gathered,
    load_sem, halo_send, halo_recv, mix_send, mix_recv, all_send, all_recv,
    fold_send, fold_recv, shift_send, shift_recv,
):
    group, tile, row = lax.axis_index("groups"), lax.axis_index("tm"), lax.axis_index("rows")
    frames, rows, columns, channels = features.shape
    depth, width = qkv_w.shape
    pdim = embed.shape[0]
    wide_all = embed.shape[1]
    blocks, block_rows = fold.shape[0], fold.shape[1]
    core = lax.rem(tile, 2)
    partners = [{"tm": tile + 1 - 2 * core}]
    if split:
        partners.append({"groups": 1 - group})
    step = 2
    while step < n_tm:
        partners.append({"tm": tile + step * (1 - 2 * lax.rem(tile // step, 2))})
        step *= 2
    reach = partners + [{"tm": lax.rem(tile + 1, n_tm)}, {"tm": lax.rem(tile + n_tm - 1, n_tm)}]
    reach += [{"rows": lax.rem(row + d, n_rows)} for d in range(1, n_rows)]

    barrier = pltpu.get_barrier_semaphore()
    for device in reach:
        pl.semaphore_signal(barrier, inc=1, device_id=device, device_id_type=MESH)

    def load(source, target, index):
        copy = pltpu.make_async_copy(source, target, load_sem.at[index])
        copy.start()
        return copy

    load_feat = load(features, feat, 0)
    load_spat = load(spatial_hbm, spat_w, 1)
    load_embed = load(embed_hbm, embed, 2)
    first = group * depth if split else 0
    load_qkv = load(qkv_hbm.at[pl.ds(pl.multiple_of(first, 16), depth)], qkv_w, 3)
    load_temp = load(temporal_hbm, temp_w, 4)
    load_head = load(head_hbm, head_w, 5)

    def remote(source, target, send, recv, device):
        return pltpu.make_async_remote_copy(
            src_ref=source, dst_ref=target, send_sem=send, recv_sem=recv,
            device_id=device, device_id_type=MESH,
        )

    up = remote(features.at[:, 0], halo.at[1], halo_send.at[0], halo_recv.at[1], {"rows": row - 1})
    down = remote(
        features.at[:, rows - 1], halo.at[0], halo_send.at[1], halo_recv.at[0], {"rows": row + 1}
    )
    has_above, has_below = row > 0, row < n_rows - 1
    has_before, has_after = tile > 0, tile < n_tm - 1

    pl.semaphore_wait(barrier, len(reach))

    @pl.when(has_above)
    def _():
        up.start()

    @pl.when(has_below)
    def _():
        down.start()

    @pl.when(jnp.logical_not(has_above))
    def _():
        halo[0] = jnp.zeros(halo.shape[1:], BF16)

    @pl.when(jnp.logical_not(has_below))
    def _():
        halo[1] = jnp.zeros(halo.shape[1:], BF16)

    @pl.when(jnp.logical_not(has_before))
    def _():
        before[...] = jnp.zeros(before.shape, BF16)

    span = 3 * channels
    column = lax.broadcasted_iota(jnp.int32, (columns, channels), 0)

    def spread_taps(values, place, frame):
        active = norm_silu(values.astype(F32))
        left = jnp.where(column == 0, 0.0, pltpu.roll(active, 1, 0))
        right = jnp.where(column == columns - 1, 0.0, pltpu.roll(active, columns - 1, 0))
        for k, shifted in enumerate((left, active, right)):
            taps[pl.ds(frame * columns, columns), pl.ds(place * span + k * channels, channels)] = (
                shifted.astype(BF16)
            )

    load_feat.wait()
    for frame in range(frames):
        for r in range(rows):
            spread_taps(feat[frame, r], r + 1, frame)
    load_spat.wait()
    inner = taps[:, span : 3 * span]
    partial[0] = dot(inner, spat_w[span : 3 * span])
    partial[1] = dot(inner, spat_w[0 : 2 * span])

    load_embed.wait()
    embedding = embed[...].astype(F32)
    mean = jnp.mean(embedding, axis=1, keepdims=True)
    if aligned:
        start = pl.multiple_of(tile * (wide_all // n_tm) + first, LANES)
        own = embed[:, pl.ds(start, depth)].astype(F32)
        scale = scale_ref[:, pl.ds(start, depth)].astype(F32)
        shift = shift_ref[:, pl.ds(start, depth)].astype(F32)
    else:
        own = part_ref[...].astype(F32)
        scale = scale_ref[...].astype(F32)
        shift = shift_ref[...].astype(F32)
    scaled = ((own - mean) * (1.0 + scale)).astype(BF16)
    rows16 = lax.broadcasted_iota(jnp.int32, (16, depth), 0)
    shift16 = jnp.where(rows16 == 0, jnp.broadcast_to(shift, (16, depth)), 0.0).astype(BF16)
    lhs = jnp.concatenate([scaled, shift16], axis=0)
    load_qkv.wait()
    chunk = width // 3
    for n in range(3):
        cols = pl.ds(n * chunk, chunk)
        terms = dot(lhs, qkv_w[:, cols])
        shifts[0, :, cols] = terms[pdim : pdim + 1]
        for b in range(blocks):
            piece = terms[b * block_rows : (b + 1) * block_rows]
            keep[b, :, cols] = piece
            part_b[b, :, cols] = piece.astype(BF16)

    half = blocks // 2
    mine = core * half + (group if split else 0)
    core_copy = remote(
        part_b.at[pl.ds((1 - core) * half, half)], core_in, fold_send.at[0], fold_recv.at[0], partners[0]
    )
    shift_copies = [
        remote(shifts.at[k], shifts_in.at[k], shift_send.at[k], shift_recv.at[k], device)
        for k, device in enumerate(partners)
    ]
    core_copy.start()
    shift_copies[0].start()

    def finish_row(r, frame_rows):
        for frame in range(frames):
            spread_taps(frame_rows[frame], 0 if r == 0 else rows + 1, frame)
        if r == 0:
            total = partial[0] + dot(taps[:, 0:span], spat_w[0:span])
        else:
            total = partial[1] + dot(taps[:, 3 * span :], spat_w[2 * span :])
        active = norm_silu(total).astype(BF16)
        for frame in range(frames):
            mixed[pl.ds(r * columns, columns), pl.ds(frame * channels, channels)] = active[
                frame * columns : (frame + 1) * columns
            ]
        copy = remote(
            mixed.at[pl.ds(r * columns, columns)], before.at[pl.ds(r * columns, columns)],
            mix_send.at[r], mix_recv.at[r], {"tm": tile + 1},
        )

        @pl.when(has_after)
        def _():
            copy.start()

        return copy

    @pl.when(has_above)
    def _():
        down.wait_recv()

    mix_copies = [finish_row(0, halo.at[0])]

    core_copy.wait()
    shift_copies[0].wait()
    cross_copies = []

    def summed(b, stage_in):
        return keep[b] + stage_in.astype(F32)

    if split:
        cross[0] = summed(core * half + 1 - group, core_in[1 - group]).astype(BF16)
        keep[mine] = summed(mine, core_in[group])
        x_in = 1
    else:
        keep[mine] = summed(mine, core_in[0])
        x_in = 0
    shifts[1] = shifts[0] + shifts_in[0]
    k = 1
    slot = 0

    def start_stage(k, slot):
        copy = remote(
            cross.at[2 * slot], cross.at[2 * slot + 1], fold_send.at[k], fold_recv.at[k], partners[k]
        )
        copy.start()
        shift_copies[k].start()
        return copy

    if not split:
        cross[0] = keep[mine].astype(BF16)
    stage = start_stage(k, slot)

    @pl.when(has_below)
    def _():
        up.wait_recv()

    mix_copies.append(finish_row(1, halo.at[1]))

    while k < len(partners):
        stage.wait()
        shift_copies[k].wait()
        keep[mine] = summed(mine, cross[2 * slot + 1])
        shifts[k + 1] = shifts[k] + shifts_in[k]
        k += 1
        slot += 1
        if k < len(partners):
            cross[2 * slot] = keep[mine].astype(BF16)
            stage = start_stage(k, slot)
    fold[mine] = keep[mine].astype(BF16)
    if split:
        share = remote(fold.at[mine], fold.at[mine], fold_send.at[k], fold_recv.at[k], partners[1])
        share.start()
        k += 1

    centred = embed[...].astype(F32) - mean
    high = centred.astype(BF16)
    wide[0:pdim] = high
    wide[pdim:] = (centred - high.astype(F32)).astype(BF16)
    products = dot_t(wide[...], wide[...])
    gram = (
        products[:pdim, :pdim] + products[:pdim, pdim:]
        + products[pdim:, :pdim] + products[pdim:, pdim:]
    ) * (1.0 / wide_all)
    for i in range(3):
        piece = gram.astype(BF16)
        gram_out[i] = piece
        gram = gram - piece.astype(F32)

    load_head.wait()
    lane = lax.broadcasted_iota(jnp.int32, (LANES, head_w.shape[0]), 0)
    latent_lane = lax.broadcasted_iota(jnp.int32, (LANES, head_w.shape[0]), 1)
    pair = PATCH * head_w.shape[0]
    heads = []
    for a in range(PATCH):
        pick = (lane >= a * pair) & (lane < (a + 1) * pair)
        pick = pick & (lax.rem(lane, head_w.shape[0]) == latent_lane)
        heads.append(dot(jnp.where(pick, 1.0, 0.0).astype(BF16), head_w[...]).astype(BF16))

    load_temp.wait()
    partial[0] = dot(mixed[:, :channels], temp_w[2 * channels :])
    partial[1] = dot(mixed[...], temp_w[channels:])

    if split:
        share.wait()
    widen = remote(
        fold.at[pl.ds(core * half, half)], fold.at[pl.ds(core * half, half)],
        fold_send.at[k], fold_recv.at[k], partners[0],
    )
    widen.start()

    @pl.when(has_before)
    def _():
        for copy in mix_copies:
            copy.wait_recv()

    for frame in range(frames):
        if frame == 0:
            total = partial[0] + dot(before[...], temp_w[: 2 * channels])
        else:
            total = partial[1] + dot(before[:, channels:], temp_w[:channels])
        total = total + jnp.concatenate([feat[frame, r].astype(F32) for r in range(rows)], axis=0)
        active = norm_silu(total).astype(BF16)
        lat[pl.ds(frame * columns, columns)] = dot_t(active[:columns], heads[0]) + dot_t(
            active[columns:], heads[1]
        )
    tokens = columns // PATCH
    out_lane = lax.broadcasted_iota(jnp.int32, (tokens, LANES), 1)
    even_lane = lax.rem(out_lane // head_w.shape[0], PATCH) == 0
    for frame in range(frames):
        even = lat[pl.ds(frame * columns, tokens, stride=PATCH), :]
        odd = lat[pl.ds(frame * columns + 1, tokens, stride=PATCH), :]
        gathered[row, frame] = jnp.where(even_lane, even, odd).astype(BF16)
    sends = [
        remote(
            gathered.at[row], gathered.at[row], all_send.at[d], all_recv.at[d],
            {"rows": lax.rem(row + d, n_rows)},
        )
        for d in range(1, n_rows)
    ]
    for copy in sends:
        copy.start()
    widen.wait()
    fold_out[...] = fold[...]
    shift_out[...] = shifts[len(partners)]
    for copy in sends:
        copy.wait()
    for p in range(n_rows):
        for frame in range(frames):
            block_out[frame, p] = gathered[p, frame]

    @pl.when(has_above)
    def _():
        up.wait_send()

    @pl.when(has_below)
    def _():
        down.wait_send()

    @pl.when(has_after)
    def _():
        for copy in mix_copies:
            copy.wait_send()


def project(pieces, block, fold, shift, gram, out, held, sems):
    pdim = fold.shape[0]
    tokens = block[:, :pdim]
    moved = dot(tokens, gram[0]) + dot(tokens, gram[1]) + dot(tokens, gram[2])
    spread = jnp.maximum(jnp.sum(moved * tokens.astype(F32), axis=-1, keepdims=True), 0.0)
    inverse = lax.rsqrt(spread + EPS)
    chunk = fold.shape[1] // pieces
    copies = []
    for n in range(pieces):
        cols = pl.ds(n * chunk, chunk)
        held[:, cols] = dot(tokens, fold[:, cols]) * inverse + shift[:, cols]
        copy = pltpu.make_async_copy(held.at[:, cols], out.at[:, cols], sems.at[n])
        copy.start()
        copies.append(copy)
    for copy in copies:
        copy.wait()


def per_device(
    n_groups, n_tm, n_rows,
    features, spatial_weight, temporal_weight, head_weight, embed_weight, ada_scale, ada_shift, qkv_weight,
):
    frames, rows, columns, channels = features.shape
    depth, width = qkv_weight.shape
    pdim, wide_all = embed_weight.shape
    latent = head_weight.shape[1]
    split = n_groups == 2
    depth = depth // 2 if split else depth
    aligned = depth % LANES == 0
    stages = n_tm.bit_length() - 1 + int(split)
    blocks = 4 if split else 2
    block_rows = pdim // blocks
    scale, shift, part = ada_scale[None], ada_shift[None], embed_weight
    if not aligned:
        start = lax.axis_index("tm") * qkv_weight.shape[0]
        if split:
            start = start + lax.axis_index("groups") * depth
        scale, shift, part = (lax.dynamic_slice_in_dim(v, start, depth, axis=1) for v in (scale, shift, part))
    hbm = pl.BlockSpec(memory_space=pl.ANY)
    vmem = pl.BlockSpec(memory_space=pltpu.VMEM)
    tokens = columns // PATCH
    dma = pltpu.SemaphoreType.DMA
    block, fold, shift_row, gram = pl.pallas_call(
        functools.partial(encode, n_groups, n_tm, n_rows, split, aligned),
        out_shape=(
            jax.ShapeDtypeStruct((frames, n_rows, tokens, LANES), BF16),
            jax.ShapeDtypeStruct((blocks, block_rows, width), BF16),
            jax.ShapeDtypeStruct((1, width), F32),
            jax.ShapeDtypeStruct((3, pdim, pdim), BF16),
        ),
        in_specs=[hbm, hbm, hbm, hbm, hbm, hbm if aligned else vmem, vmem, vmem, hbm],
        out_specs=(vmem, vmem, vmem, vmem),
        scratch_shapes=[
            pltpu.VMEM(features.shape, BF16),
            pltpu.VMEM((2, frames, columns, channels), BF16),
            pltpu.VMEM((frames * columns, (rows + 2) * 3 * channels), BF16),
            pltpu.VMEM((9 * channels, channels), BF16),
            pltpu.VMEM((3 * channels, channels), BF16),
            pltpu.VMEM((latent, channels), BF16),
            pltpu.VMEM((pdim, wide_all), BF16),
            pltpu.VMEM((2 * pdim, wide_all), BF16),
            pltpu.VMEM((depth, width), BF16),
            pltpu.VMEM((rows * columns, frames * channels), BF16),
            pltpu.VMEM((rows * columns, frames * channels), BF16),
            pltpu.VMEM((2, frames * columns, channels), F32),
            pltpu.VMEM((frames * columns, LANES), F32),
            pltpu.VMEM((blocks, block_rows, width), BF16),
            pltpu.VMEM((blocks // 2, block_rows, width), BF16),
            pltpu.VMEM((blocks, block_rows, width), F32),
            pltpu.VMEM((2 * (stages - 1), block_rows, width), BF16),
            pltpu.VMEM((blocks, block_rows, width), BF16),
            pltpu.VMEM((stages + 1, 1, width), F32),
            pltpu.VMEM((stages, 1, width), F32),
            pltpu.VMEM((n_rows, frames, tokens, LANES), BF16),
            dma((6,)),
            dma((2,)), dma((2,)),
            dma((rows,)), dma((rows,)),
            dma((n_rows,)), dma((n_rows,)),
            dma((stages + 2,)), dma((stages + 2,)),
            dma((stages,)), dma((stages,)),
        ],
        compiler_params=pltpu.CompilerParams(
            collective_id=0, has_side_effects=True, vmem_limit_bytes=56 * 2**20
        ),
        name="encode",
    )(
        features,
        spatial_weight.reshape(9 * channels, channels),
        temporal_weight.reshape(3 * channels, channels),
        head_weight.T,
        embed_weight,
        part,
        scale,
        shift,
        qkv_weight,
    )
    count = frames * n_rows * tokens
    pieces = 3
    return pl.pallas_call(
        functools.partial(project, pieces),
        out_shape=jax.ShapeDtypeStruct((count, width), F32),
        in_specs=[vmem] * 4,
        out_specs=hbm,
        scratch_shapes=[pltpu.VMEM((count, width), F32), dma((pieces,))],
        compiler_params=pltpu.CompilerParams(vmem_limit_bytes=32 * 2**20),
        name="project",
    )(block.reshape(count, LANES), fold.reshape(pdim, width), shift_row, gram)


def solution(mesh):
    return jax.shard_map(
        functools.partial(per_device, mesh.shape["groups"], mesh.shape["tm"], mesh.shape["rows"]),
        mesh=mesh,
        in_specs=(
            P(("groups", "tm"), "rows", None, None),
            P(),
            P(),
            P(),
            P(),
            P(),
            P(),
            P("tm", "rows"),
        ),
        out_specs=P(("groups", "tm"), "rows"),
        check_vma=False,
    )
```

time: 49.8 us -> 37.4 us (0.75)
  Pallas kernels: 0 us -> 31 us
  starting transfers between devices: 14.8 us -> 0 us
  blocking collectives: 13.5 us -> 0 us
  matrix products: 12.9 us -> 0 us
  other arithmetic: 3.92 us -> 0 us
  local copies, waits for them, and re-layouts: 2.46 us -> 5.97 us
  waiting for transfers between devices: 1.57 us -> 0 us
    pallas_call x0 -> x2, Pallas kernels: none -> 31 us  [the longest x1 28.8 us: per_device(): pl.pallas_call(functools.partial(encode, n_groups, n_tm, n_rows, split, a...]
    ppermute x5 -> x0, starting transfers between devices: 14.8 us -> none  [the longest x2 7.07 us: summed_over(): lax.ppermute(values, axis, [(i, i ^ step) for i in range(count)])]
    all_gather x1 -> x0, blocking collectives: 13.5 us -> none  [per_device(): token_block = lax.all_gather(patches, 'rows', axis=1, tiled=True)]
    dot_general x17 -> x0, matrix products: 12.9 us -> none  [the longest x1 3.81 us: per_device(): jnp.dot(jnp.concatenate([*halves(scaled), shift[None]], axis=0), qkv_weig...]
    unnamed x14 -> x8, local copies, waits for them, and re-layouts: 0.59 us -> 3.34 us
    broadcast_in_dim x1 -> x2, local copies, waits for them, and re-layouts: 0.01 us -> 2.63 us  [per_device(): scale, shift, part = (ada_scale[None], ada_shift[None], embed_weight)]
    convert_element_type x4 -> x0, other arithmetic: 1.68 us -> none  [the longest x1 1.28 us: per_device(): activated = norm_silu(features.astype(jnp.float32)).astype(jnp.bfloat16)]
    ppermute x5 -> x0, waiting for transfers between devices: 1.57 us -> none  [the longest x1 1.56 us: with_halo(): lax.ppermute(head, axis, [((i + 1) % count, i) for i in range(ends)])]
  transfers between devices with their start and end apart: 5 -> 0, of which waited for: 1 -> 0; matrix products, arithmetic and copies ran while one was open for 27% -> 0% of each run, Pallas kernels for 0% -> 0%
where the time goes in v1:
time: 37.4 us; the launch traced here: 37 us
  Pallas kernels  31 us (83%)
  local copies, waits for them, and re-layouts  5.97 us (16%)
    pallas_call x1, Pallas kernels, per_device(): pl.pallas_call(functools.partial(encode, n_groups, n_tm, n_rows, split, a...  28.8 us
    unnamed x8, local copies, waits for them, and re-layouts  3.34 us
    broadcast_in_dim x2, local copies, waits for them, and re-layouts, per_device(): scale, shift, part = (ada_scale[None], ada_shift[None], embed_weight)  2.63 us
    pallas_call x1, Pallas kernels, per_device(): pl.pallas_call(functools.partial(project, pieces), out_shape=jax.ShapeDty...  2.24 us

profile of v1, /device:TPU:0, one launch (start us, length us, event | category | flops | bytes accessed | tf_op | source)
XLA Modules:
  0.0 37.0 jit_solution(5640249544682917673)
XLA Ops:
  0.0 1.3 %broadcast_in_dim.6.scale_ref = bf16[1,5120]{1,0:T(2,128)(2,1)} reshape(bf16[5120]{0:T(1024)(128)(2,1)} %param.13) | data formatting | bytes 20480 | tf_op jit(solution)/shard_map/broadcast_in_dim | solution.py:373
  1.3 1.3 %broadcast_in_dim.7.shift_ref = bf16[1,5120]{1,0:T(2,128)(2,1)} reshape(bf16[5120]{0:T(1024)(128)(2,1)} %param.14) | data formatting | bytes 20480 | tf_op jit(solution)/shard_map/broadcast_in_dim | solution.py:373
  2.6 28.8 %encode.1 = (bf16[2,4,48,128]{3,2,1,0:T(8,128)(2,1)}, bf16[4,16,2304]{2,1,0:T(8,128)(2,1)}, f32[1,2304]{1,0:T(1,128)}, bf16[3,64,64]{2,1,0:T(8,128)(2,1)}) custom-call(bf16[2,2,96,512]{3,2,1,0:T(8,128)(2,1)} %features.1, bf16[4608,512]{1,0:T(8,128)(2,1)} %bitcast.7, bf16[1536,512]{1,0:T(8,128)(2,1)} %bitcast.8, bf16[16,512]{1,0:T(8,128)(2,1)} %bitcast.9, ...), custom_call_target="tpu_custom_call" | custom-call | tf_op jit(solution)/shard_map/encode/pallas_call | solution.py:383
  31.4 0.0 copy-start
  31.4 1.0 %copy-done = bf16[4,16,2304]{2,1,0:T(8,128)(2,1)S(1)} copy-done((bf16[4,16,2304]{2,1,0:T(8,128)(2,1)S(1)}, bf16[4,16,2304]{2,1,0:T(8,128)(2,1)}, u32[]{:S(2)}) %copy-start) | copy-done | bytes 294936
  32.4 0.0 copy-start.1
  32.4 0.9 %copy-done.1 = bf16[2,4,48,128]{3,2,1,0:T(8,128)(2,1)S(1)} copy-done((bf16[2,4,48,128]{3,2,1,0:T(8,128)(2,1)S(1)}, bf16[2,4,48,128]{3,2,1,0:T(8,128)(2,1)}, u32[]{:S(2)}) %copy-start.1) | copy-done | bytes 98328
  33.3 0.0 copy-start.2
  33.3 0.8 %copy-done.2 = bf16[3,64,64]{2,1,0:T(8,128)(2,1)S(1)} copy-done((bf16[3,64,64]{2,1,0:T(8,128)(2,1)S(1)}, bf16[3,64,64]{2,1,0:T(8,128)(2,1)}, u32[]{:S(2)}) %copy-start.2) | copy-done | bytes 24600
  34.1 0.0 copy-start.3
  34.1 0.7 %copy-done.3 = f32[1,2304]{1,0:T(1,128)S(1)} copy-done((f32[1,2304]{1,0:T(1,128)S(1)}, f32[1,2304]{1,0:T(1,128)}, u32[]{:S(2)}) %copy-start.3) | copy-done | bytes 9240
  34.8 2.2 %project.1 = f32[384,2304]{1,0:T(8,128)} custom-call(bf16[384,128]{1,0:T(8,128)(2,1)S(1)} %bitcast.6, bf16[64,2304]{1,0:T(8,128)(2,1)S(1)} %bitcast.5, f32[1,2304]{1,0:T(1,128)S(1)} %copy-done.3, bf16[3,64,64]{2,1,0:T(8,128)(2,1)S(1)} %copy-done.2), custom_call_target="tpu_custom_call" | custom-call | tf_op jit(solution)/shard_map/project/pallas_call | solution.py:439
Async XLA Ops:
  31.4 1.0 %copy-start = (bf16[4,16,2304]{2,1,0:T(8,128)(2,1)S(1)}, bf16[4,16,2304]{2,1,0:T(8,128)(2,1)}, u32[]{:S(2)}) copy-start(bf16[4,16,2304]{2,1,0:T(8,128)(2,1)} %get-tuple-element.10) | copy-start | bytes 884740
  32.4 0.9 %copy-start.1 = (bf16[2,4,48,128]{3,2,1,0:T(8,128)(2,1)S(1)}, bf16[2,4,48,128]{3,2,1,0:T(8,128)(2,1)}, u32[]{:S(2)}) copy-start(bf16[2,4,48,128]{3,2,1,0:T(8,128)(2,1)} %get-tuple-element.9) | copy-start | bytes 294916
  33.3 0.8 %copy-start.2 = (bf16[3,64,64]{2,1,0:T(8,128)(2,1)S(1)}, bf16[3,64,64]{2,1,0:T(8,128)(2,1)}, u32[]{:S(2)}) copy-start(bf16[3,64,64]{2,1,0:T(8,128)(2,1)} %get-tuple-element.12.gram) | copy-start | bytes 73732
  34.1 0.7 %copy-start.3 = (f32[1,2304]{1,0:T(1,128)S(1)}, f32[1,2304]{1,0:T(1,128)}, u32[]{:S(2)}) copy-start(f32[1,2304]{1,0:T(1,128)} %get-tuple-element.11.shift) | copy-start | bytes 27652

commit v2 on v1

--- a/solution.py
+++ b/solution.py
@@ -34,7 +34,7 @@
     features, spatial_hbm, temporal_hbm, head_hbm, embed_hbm, part_ref, scale_ref, shift_ref, qkv_hbm,
     block_out, fold_out, shift_out, gram_out,
     feat, halo, taps, spat_w, temp_w, head_w, embed, wide, qkv_w, mixed, before, partial, lat,
-    part_b, core_in, keep, cross, fold, shifts, shifts_in, gathered,
+    part_b, core_in, keep, cross, fold, shifts, shifts_in, gathered, vectors,
     load_sem, halo_send, halo_recv, mix_send, mix_recv, all_send, all_recv,
     fold_send, fold_recv, shift_send, shift_recv,
 ):
@@ -134,8 +134,13 @@
     if aligned:
         start = pl.multiple_of(tile * (wide_all // n_tm) + first, LANES)
         own = embed[:, pl.ds(start, depth)].astype(F32)
-        scale = scale_ref[:, pl.ds(start, depth)].astype(F32)
-        shift = shift_ref[:, pl.ds(start, depth)].astype(F32)
+        vectors[0] = scale_ref[...].astype(F32)
+        vectors[1] = shift_ref[...].astype(F32)
+        at = start // LANES
+        scale, shift = (
+            jnp.concatenate([vectors[v, pl.ds(at + j, 1)] for j in range(depth // LANES)], axis=1)
+            for v in range(2)
+        )
     else:
         own = part_ref[...].astype(F32)
         scale = scale_ref[...].astype(F32)
@@ -370,8 +375,10 @@
     stages = n_tm.bit_length() - 1 + int(split)
     blocks = 4 if split else 2
     block_rows = pdim // blocks
-    scale, shift, part = ada_scale[None], ada_shift[None], embed_weight
+    part = embed_weight
+    scale, shift = (v.reshape(wide_all // LANES, LANES) for v in (ada_scale, ada_shift))
     if not aligned:
+        scale, shift = ada_scale[None], ada_shift[None]
         start = lax.axis_index("tm") * qkv_weight.shape[0]
         if split:
             start = start + lax.axis_index("groups") * depth
@@ -383,10 +390,10 @@
     block, fold, shift_row, gram = pl.pallas_call(
         functools.partial(encode, n_groups, n_tm, n_rows, split, aligned),
         out_shape=(
-            jax.ShapeDtypeStruct((frames, n_rows, tokens, LANES), BF16),
-            jax.ShapeDtypeStruct((blocks, block_rows, width), BF16),
-            jax.ShapeDtypeStruct((1, width), F32),
-            jax.ShapeDtypeStruct((3, pdim, pdim), BF16),
+            pltpu.VMEM((frames, n_rows, tokens, LANES), BF16),
+            pltpu.VMEM((blocks, block_rows, width), BF16),
+            pltpu.VMEM((1, width), F32),
+            pltpu.VMEM((3, pdim, pdim), BF16),
         ),
         in_specs=[hbm, hbm, hbm, hbm, hbm, hbm if aligned else vmem, vmem, vmem, hbm],
         out_specs=(vmem, vmem, vmem, vmem),
@@ -412,6 +419,7 @@
             pltpu.VMEM((stages + 1, 1, width), F32),
             pltpu.VMEM((stages, 1, width), F32),
             pltpu.VMEM((n_rows, frames, tokens, LANES), BF16),
+            pltpu.VMEM((2, wide_all // LANES, LANES), F32),
             dma((6,)),
             dma((2,)), dma((2,)),
             dma((rows,)), dma((rows,)),

time: 37.4 us -> 30.5 us (0.82)
  local copies, waits for them, and re-layouts: 5.97 us -> 0 us
  Pallas kernels: 31 us -> 30.2 us
    unnamed x8 -> x0, local copies, waits for them, and re-layouts: 3.34 us -> none
    broadcast_in_dim x2 -> x0, local copies, waits for them, and re-layouts: 2.63 us -> none  [per_device(): scale, shift, part = (ada_scale[None], ada_shift[None], embed_weight)]
    pallas_call x1, Pallas kernels: 28.8 us -> 28 us  [per_device(): pl.pallas_call(functools.partial(encode, n_groups, n_tm, n_rows, split, a...]
where the time goes in v2:
time: 30.5 us; the launch traced here: 30.2 us
  Pallas kernels  30.2 us (99%)
    pallas_call x1, Pallas kernels, per_device(): pl.pallas_call(functools.partial(encode, n_groups, n_tm, n_rows, split, a...  28 us
    pallas_call x1, Pallas kernels, per_device(): pl.pallas_call(functools.partial(project, pieces), out_shape=jax.ShapeDty...  2.24 us

profile of v2, /device:TPU:0, one launch (start us, length us, event | category | flops | bytes accessed | tf_op | source)
XLA Modules:
  0.0 30.2 jit_solution(18222072946118176266)
XLA Ops:
  0.0 28.0 %encode.1 = (bf16[2,4,48,128]{3,2,1,0:T(8,128)(2,1)S(1)}, bf16[4,16,2304]{2,1,0:T(8,128)(2,1)S(1)}, f32[1,2304]{1,0:T(1,128)S(1)}, bf16[3,64,64]{2,1,0:T(8,128)(2,1)S(1)}) custom-call(bf16[2,2,96,512]{3,2,1,0:T(8,128)(2,1)} %features.1, bf16[4608,512]{1,0:T(8,128)(2,1)} %bitcast.9, bf16[1536,512]{1,0:T(8,128)(2,1)} %bitcast.10, bf16[16,512]{1,0:T(8,128)(2,1)} %bitcast.11, ...), custom_call_target="tpu_custom_call" | custom-call | tf_op jit(solution)/shard_map/encode/pallas_call | solution.py:390
  28.0 2.2 %project.1 = f32[384,2304]{1,0:T(8,128)} custom-call(bf16[384,128]{1,0:T(8,128)(2,1)S(1)} %bitcast.8, bf16[64,2304]{1,0:T(8,128)(2,1)S(1)} %bitcast.7, f32[1,2304]{1,0:T(1,128)S(1)} %get-tuple-element.11.shift, bf16[3,64,64]{2,1,0:T(8,128)(2,1)S(1)} %get-tuple-element.12.gram), custom_call_target="tpu_custom_call" | custom-call | tf_op jit(solution)/shard_map/project/pallas_call | solution.py:447

commit v3 on v2

v3 whole, which is shorter than its diff:
```python
import functools

import jax
import jax.numpy as jnp
from jax import lax
from jax.experimental import pallas as pl
from jax.experimental.pallas import tpu as pltpu
from jax.sharding import PartitionSpec as P

MESH = pl.DeviceIdType.MESH
PATCH = 2
LANES = 128
EPS = 1e-06
F32 = jnp.float32
BF16 = jnp.bfloat16


def dot(a, b):
    return jnp.dot(a, b, preferred_element_type=F32)


def dot_t(a, b):
    return lax.dot_general(a, b, (((1,), (1,)), ((), ())), preferred_element_type=F32)


def norm_silu(values):
    scaled = values * lax.rsqrt(jnp.mean(values * values, axis=-1, keepdims=True) + EPS)
    half = 0.5 * scaled
    return half + half * jnp.tanh(half)


def encode(
    n_tm, n_rows, split, aligned,
    features, spatial_hbm, temporal_hbm, head_hbm, embed_hbm, part_hbm, scale_hbm, shift_hbm, qkv_hbm,
    block_out, fold_out, shift_out, gram_out,
    feat, halo, taps, spat_w, temp_w, head_w, embed, part, scale_v, shift_v, vectors, wide, qkv_w,
    mixed, before, partial, lat, part_b, core_in, keep, cross, quad_in, stage, fold, shifts, shifts_in, gathered, heads,
    load_sem, halo_send, halo_recv, mix_send, mix_recv, all_send, all_recv,
    fold_send, fold_recv, shift_send, shift_recv, relay,
):
    group, tile, row = lax.axis_index("groups"), lax.axis_index("tm"), lax.axis_index("rows")
    frames, rows, columns, channels = features.shape
    depth, width = qkv_w.shape
    pdim, wide_all = embed.shape
    latent = head_w.shape[0]
    _, quads, block_rows, _ = fold.shape
    has_above, has_below = row > 0, row < n_rows - 1
    has_before, has_after = tile > 0, tile < n_tm - 1
    near = [({"rows": row - 1}, has_above), ({"rows": row + 1}, has_below)]
    count_rows = has_above.astype(jnp.int32) + has_below.astype(jnp.int32)
    count_tiles = has_before.astype(jnp.int32) + has_after.astype(jnp.int32)
    core = lax.rem(tile, 2)
    other_core = {"tm": tile + 1 - 2 * core}

    def flipped(bit):
        return tile + bit * (1 - 2 * lax.rem(tile // bit, 2))

    bits = [("tm", lax.rem(tile // 2, 2), flipped(2))] if n_tm >= 4 else []
    if split:
        bits.append(("groups", group, 1 - group))
    mine = sum((bit[1] * 2**n for n, bit in enumerate(bits)), 0)
    direct = []
    for mask in range(1, quads):
        chosen = [n for n in range(len(bits)) if mask >> n & 1]
        place = mine + sum(2**n * (1 - 2 * bits[n][1]) for n in chosen)
        direct.append(({bits[n][0]: bits[n][2] for n in chosen}, place))
    later = []
    step = 4
    while step < n_tm:
        later.append({"tm": flipped(step)})
        step *= 2
    partners = [other_core] + [device for device, _ in direct] + later

    def signal(sem, device):
        pl.semaphore_signal(sem, inc=1, device_id=device, device_id_type=MESH)

    barrier = pltpu.get_barrier_semaphore()
    for device in partners:
        signal(barrier, device)
    for device, there in near + [({"tm": tile - 1}, has_before), ({"tm": tile + 1}, has_after)]:

        @pl.when(there)
        def _():
            signal(barrier, device)

    def load(source, target, index):
        copy = pltpu.make_async_copy(source, target, load_sem.at[index])
        copy.start()
        return copy

    first = group * depth if split else 0
    load_feat = load(features, feat, 0)
    load_embed = load(embed_hbm, embed, 1)
    load_scale = load(scale_hbm, scale_v, 2)
    load_shift = load(shift_hbm, shift_v, 3)
    if not aligned:
        load_part = load(part_hbm, part, 4)
    load_qkv = load(qkv_hbm.at[pl.ds(pl.multiple_of(first, 16), depth)], qkv_w, 5)
    load_spat = load(spatial_hbm, spat_w, 6)
    load_temp = load(temporal_hbm, temp_w, 7)
    load_head = load(head_hbm, head_w, 8)

    def remote(source, target, send, recv, device):
        return pltpu.make_async_remote_copy(
            src_ref=source, dst_ref=target, send_sem=send, recv_sem=recv,
            device_id=device, device_id_type=MESH,
        )

    ups, downs = [], []
    for f in range(frames):
        ups.append(
            remote(features.at[f, 0], halo.at[f, 1], halo_send.at[f, 0], halo_recv.at[f, 1], near[0][0])
        )
        downs.append(
            remote(
                features.at[f, rows - 1], halo.at[f, 0], halo_send.at[f, 1], halo_recv.at[f, 0], near[1][0]
            )
        )

    pl.semaphore_wait(barrier, len(partners) + count_rows + count_tiles)
    for f in range(frames):

        @pl.when(has_above)
        def _():
            ups[f].start()

        @pl.when(has_below)
        def _():
            downs[f].start()

    phases = max(n_rows - 2, 0)
    done_phases = [0]

    def tell(phase):
        if phase < phases:
            for device, there in near:

                @pl.when(there)
                def _():
                    signal(relay.at[phase], device)

    def next_phase():
        phase = done_phases[0]
        if phase < phases:
            pl.semaphore_wait(relay.at[phase], count_rows)
            tell(phase + 1)
            done_phases[0] = phase + 1

    tell(0)

    @pl.when(jnp.logical_not(has_above))
    def _():
        for f in range(frames):
            halo[f, 0] = jnp.zeros(halo.shape[2:], BF16)

    @pl.when(jnp.logical_not(has_below))
    def _():
        for f in range(frames):
            halo[f, 1] = jnp.zeros(halo.shape[2:], BF16)

    @pl.when(jnp.logical_not(has_before))
    def _():
        before[...] = jnp.zeros(before.shape, BF16)

    span = 3 * channels
    column = lax.broadcasted_iota(jnp.int32, (columns, channels), 0)

    def spread_taps(values, place, frame):
        active = norm_silu(values.astype(F32))
        left = jnp.where(column == 0, 0.0, pltpu.roll(active, 1, 0))
        right = jnp.where(column == columns - 1, 0.0, pltpu.roll(active, columns - 1, 0))
        for k, shifted in enumerate((left, active, right)):
            taps[pl.ds(frame * columns, columns), pl.ds(place * span + k * channels, channels)] = (
                shifted.astype(BF16)
            )

    load_embed.wait()
    load_scale.wait()
    load_shift.wait()
    mean = jnp.mean(embed[...].astype(F32), axis=1, keepdims=True)
    if aligned:
        start = pl.multiple_of(tile * (wide_all // n_tm) + first, LANES)
        own = embed[:, pl.ds(start, depth)].astype(F32)
        vectors[0] = scale_v[...].astype(F32)
        vectors[1] = shift_v[...].astype(F32)
        at = start // LANES
        scale, shift = (
            jnp.concatenate([vectors[v, pl.ds(at + j, 1)] for j in range(depth // LANES)], axis=1)
            for v in range(2)
        )
    else:
        load_part.wait()
        own, scale, shift = part[...].astype(F32), scale_v[...].astype(F32), shift_v[...].astype(F32)
    scaled = ((own - mean) * (1.0 + scale)).astype(BF16)
    rows16 = lax.broadcasted_iota(jnp.int32, (16, depth), 0)
    shift16 = jnp.where(rows16 == 0, jnp.broadcast_to(shift, (16, depth)), 0.0).astype(BF16)
    lhs = jnp.concatenate([scaled, shift16], axis=0)
    load_qkv.wait()
    chunk = width // 3
    for n in range(3):
        cols = pl.ds(n * chunk, chunk)
        terms = dot(lhs, qkv_w[:, cols])
        shifts[0, :, cols] = terms[pdim : pdim + 1]
        for side in range(2):
            for b in range(quads):
                low = (side * quads + b) * block_rows
                piece = terms[low : low + block_rows]
                keep[side, b, :, cols] = piece
                part_b[side, b, :, cols] = piece.astype(BF16)

    core_copies = [
        remote(part_b.at[1 - core], core_in, fold_send.at[0], fold_recv.at[0], other_core),
        remote(shifts.at[0], shifts_in.at[0], shift_send.at[0], shift_recv.at[0], other_core),
    ]
    for copy in core_copies:
        copy.start()

    load_feat.wait()
    for f in range(frames):
        for r in range(rows):
            spread_taps(feat[f, r], r + 1, f)
    load_spat.wait()
    inner = taps[:, span : 3 * span]
    direct_copies = []
    for r in range(rows):
        total = dot(inner, spat_w[(1 - r) * span : (3 - r) * span])
        for f in range(frames):
            partial[f, pl.ds(r * columns, columns)] = total[f * columns : (f + 1) * columns]
        if r == 0:
            for copy in core_copies:
                copy.wait()
            shifts[1] = shifts[0] + shifts_in[0]
            for b in range(quads):
                cross[b] = (keep[core, b] + core_in[b].astype(F32)).astype(BF16)
            for m, (device, place) in enumerate(direct, 1):
                direct_copies += [
                    remote(cross.at[place], quad_in.at[m], fold_send.at[m], fold_recv.at[m], device),
                    remote(shifts.at[1], shifts_in.at[m], shift_send.at[m], shift_recv.at[m], device),
                ]
            for copy in direct_copies:
                copy.start()
    next_phase()

    def finish_frame(f):
        @pl.when(has_above)
        def _():
            downs[f].wait_recv()

        @pl.when(has_below)
        def _():
            ups[f].wait_recv()

        spread_taps(halo[f, 0], 0, f)
        spread_taps(halo[f, 1], rows + 1, f)
        here = pl.ds(f * columns, columns)
        copies = []
        for r, (place, weights) in enumerate(
            ((0, spat_w[0:span]), (3 * span, spat_w[2 * span : 3 * span]))
        ):
            lines = pl.ds(r * columns, columns)
            total = partial[f, lines] + dot(taps[here, pl.ds(place, span)], weights)
            mixed[f, lines] = norm_silu(total).astype(BF16)
            copies.append(
                remote(
                    mixed.at[f, lines], before.at[f, lines], mix_send.at[f, r], mix_recv.at[f, r],
                    {"tm": tile + 1},
                )
            )

            @pl.when(has_after)
            def _():
                copies[-1].start()

        return copies

    mix_copies = finish_frame(0)
    next_phase()
    mix_copies += finish_frame(1)
    next_phase()

    load_head.wait()
    lane = lax.broadcasted_iota(jnp.int32, (latent, LANES), 1)
    latent_lane = lax.broadcasted_iota(jnp.int32, (latent, LANES), 0)
    pair = PATCH * latent
    for f in range(frames):
        for a in range(PATCH):
            low = f * pdim + a * pair
            pick = (lane >= low) & (lane < low + pair) & (lax.rem(lane, latent) == latent_lane)
            spread_head = lax.dot_general(
                head_w[...], jnp.where(pick, 1.0, 0.0).astype(BF16), (((0,), (0,)), ((), ())),
                preferred_element_type=F32,
            )
            heads[PATCH * f + a] = spread_head.astype(BF16)
    load_temp.wait()
    partial[0] = dot(mixed[0], temp_w[2 * channels :])
    partial[1] = dot(jnp.concatenate([mixed[0], mixed[1]], axis=1), temp_w[channels:])

    total = keep[core, mine] + core_in[mine].astype(F32)
    shift_total = shifts[1]
    for copy in direct_copies:
        copy.wait()
    for m in range(1, quads):
        total = total + quad_in[m].astype(F32)
        shift_total = shift_total + shifts_in[m]
    for n, device in enumerate(later):
        stage[2 * n] = total.astype(BF16)
        shifts[2 + n] = shift_total
        pair_copies = [
            remote(
                stage.at[2 * n], stage.at[2 * n + 1], fold_send.at[quads + n], fold_recv.at[quads + n], device
            ),
            remote(
                shifts.at[2 + n], shifts_in.at[quads + n],
                shift_send.at[quads + n], shift_recv.at[quads + n], device,
            ),
        ]
        for copy in pair_copies:
            copy.start()
        for copy in pair_copies:
            copy.wait()
        total = total + stage[2 * n + 1].astype(F32)
        shift_total = shift_total + shifts_in[quads + n]
    fold[core, mine] = total.astype(BF16)
    shift_out[...] = shift_total
    base = quads + len(later)
    shares = []

    def share_next():
        n = len(shares)
        if n < len(bits):
            known = fold.at[core, pl.ds(mine - lax.rem(mine, 2**n), 2**n)]
            copy = remote(
                known, known, fold_send.at[base + n], fold_recv.at[base + n], {bits[n][0]: bits[n][2]}
            )
            copy.start()
            shares.append(copy)

    share_next()

    centred = embed[...].astype(F32) - mean
    high = centred.astype(BF16)
    wide[0:pdim] = high
    wide[pdim:] = (centred - high.astype(F32)).astype(BF16)
    products = dot_t(wide[...], wide[...])
    gram = (
        products[:pdim, :pdim] + products[:pdim, pdim:]
        + products[pdim:, :pdim] + products[pdim:, pdim:]
    ) * (1.0 / wide_all)
    for i in range(3):
        piece = gram.astype(BF16)
        gram_out[i] = piece
        gram = gram - piece.astype(F32)

    @pl.when(has_before)
    def _():
        for copy in mix_copies[:rows]:
            copy.wait_recv()

    partial[0] = partial[0] + dot(before[0], temp_w[:channels])
    while done_phases[0] < phases:
        next_phase()

    @pl.when(has_before)
    def _():
        for copy in mix_copies[rows:]:
            copy.wait_recv()

    for f in range(frames):
        total = partial[f] + dot(before[1], temp_w[(1 - f) * channels : (2 - f) * channels])
        total = total + jnp.concatenate([feat[f, r].astype(F32) for r in range(rows)], axis=0)
        active = norm_silu(total).astype(BF16)
        term = dot(active[:columns], heads[PATCH * f]) + dot(active[columns:], heads[PATCH * f + 1])
        lat[...] = term if f == 0 else lat[...] + term
    tokens = columns // PATCH
    out_lane = lax.broadcasted_iota(jnp.int32, (tokens, LANES), 1)
    even = lat[pl.ds(0, tokens, stride=PATCH), :]
    odd = lat[pl.ds(1, tokens, stride=PATCH), :]
    gathered[row] = jnp.where(lax.rem(out_lane // latent, PATCH) == 0, even, odd).astype(BF16)
    sends = [
        remote(
            gathered.at[row], gathered.at[row], all_send.at[d], all_recv.at[d],
            {"rows": lax.rem(row + d, n_rows)},
        )
        for d in range(1, n_rows)
    ]
    for copy in sends:
        copy.start()
    for n in range(len(bits)):
        shares[n].wait()
        share_next()
    base += len(bits)
    widen = remote(fold.at[core], fold.at[core], fold_send.at[base], fold_recv.at[base], other_core)
    widen.start()

    @pl.when(has_above)
    def _():
        for copy in ups:
            copy.wait_send()

    @pl.when(has_below)
    def _():
        for copy in downs:
            copy.wait_send()

    @pl.when(has_after)
    def _():
        for copy in mix_copies:
            copy.wait_send()

    widen.wait()
    fold_out[...] = fold[...]
    for copy in sends:
        copy.wait()
    block_out[...] = gathered[...]


def project(n_rows, frames, block, fold, shift, gram, out, held, sems):
    pdim, width = fold.shape
    tokens = block.shape[1]
    lane = lax.broadcasted_iota(jnp.int32, (n_rows * tokens, LANES), 1)
    weights = jnp.concatenate([fold[...]] * frames, axis=0)
    quadratic = [jnp.concatenate([gram[i]] * frames, axis=0) for i in range(3)]
    everything = block[...].reshape(n_rows * tokens, LANES)
    parts = 4
    lines = n_rows * tokens // parts
    copies = []
    for f in range(frames):
        own = (lane >= f * pdim) & (lane < (f + 1) * pdim)
        packed = jnp.where(own, everything.astype(F32), 0.0)
        patches = packed.astype(BF16)
        for n in range(parts):
            mine = patches[n * lines : (n + 1) * lines]
            moved = dot(mine, quadratic[0]) + dot(mine, quadratic[1]) + dot(mine, quadratic[2])
            sides = packed[n * lines : (n + 1) * lines, f * pdim : (f + 1) * pdim]
            spread = jnp.maximum(jnp.sum(moved * sides, axis=-1, keepdims=True), 0.0)
            here = pl.ds((f * parts + n) * lines, lines)
            held[here] = dot(mine, weights) * lax.rsqrt(spread + EPS) + shift[...]
            copy = pltpu.make_async_copy(held.at[here], out.at[here], sems.at[f * parts + n])
            copy.start()
            copies.append(copy)
    for copy in copies:
        copy.wait()


def per_device(
    n_groups, n_tm, n_rows,
    features, spatial_weight, temporal_weight, head_weight, embed_weight, ada_scale, ada_shift, qkv_weight,
):
    frames, rows, columns, channels = features.shape
    depth, width = qkv_weight.shape
    pdim, wide_all = embed_weight.shape
    latent = head_weight.shape[1]
    split = n_groups == 2
    depth = depth // 2 if split else depth
    aligned = depth % LANES == 0
    quads = (2 if split else 1) * (2 if n_tm >= 4 else 1)
    later = max(n_tm.bit_length() - 3, 0)
    block_rows = pdim // (2 * quads)
    fold_shape = (2, quads, block_rows, width)
    part = embed_weight
    scale, shift = (v.reshape(wide_all // LANES, LANES) for v in (ada_scale, ada_shift))
    if not aligned:
        scale, shift = ada_scale[None], ada_shift[None]
        start = lax.axis_index("tm") * qkv_weight.shape[0]
        if split:
            start = start + lax.axis_index("groups") * depth
        scale, shift, part = (lax.dynamic_slice_in_dim(v, start, depth, axis=1) for v in (scale, shift, part))
    hbm = pl.BlockSpec(memory_space=pl.ANY)
    vmem = pl.BlockSpec(memory_space=pltpu.VMEM)
    tokens = columns // PATCH
    dma = pltpu.SemaphoreType.DMA
    block, fold, shift_row, gram = pl.pallas_call(
        functools.partial(encode, n_tm, n_rows, split, aligned),
        out_shape=(
            pltpu.VMEM((n_rows, tokens, LANES), BF16),
            pltpu.VMEM(fold_shape, BF16),
            pltpu.VMEM((1, width), F32),
            pltpu.VMEM((3, pdim, pdim), BF16),
        ),
        in_specs=[hbm] * 9,
        out_specs=(vmem, vmem, vmem, vmem),
        scratch_shapes=[
            pltpu.VMEM(features.shape, BF16),
            pltpu.VMEM((frames, 2, columns, channels), BF16),
            pltpu.VMEM((frames * columns, (rows + 2) * 3 * channels), BF16),
            pltpu.VMEM((9 * channels, channels), BF16),
            pltpu.VMEM((3 * channels, channels), BF16),
            pltpu.VMEM((latent, channels), BF16),
            pltpu.VMEM((pdim, wide_all), BF16),
            pltpu.VMEM((pdim, depth), BF16),
            pltpu.VMEM(scale.shape, BF16),
            pltpu.VMEM(shift.shape, BF16),
            pltpu.VMEM((2, wide_all // LANES, LANES), F32),
            pltpu.VMEM((2 * pdim, wide_all), BF16),
            pltpu.VMEM((depth, width), BF16),
            pltpu.VMEM((frames, rows * columns, channels), BF16),
            pltpu.VMEM((frames, rows * columns, channels), BF16),
            pltpu.VMEM((frames, rows * columns, channels), F32),
            pltpu.VMEM((columns, LANES), F32),
            pltpu.VMEM(fold_shape, BF16),
            pltpu.VMEM(fold_shape[1:], BF16),
            pltpu.VMEM(fold_shape, F32),
            pltpu.VMEM(fold_shape[1:], BF16),
            pltpu.VMEM(fold_shape[1:], BF16),
            pltpu.VMEM((max(2 * later, 1), block_rows, width), BF16),
            pltpu.VMEM(fold_shape, BF16),
            pltpu.VMEM((2 + later, 1, width), F32),
            pltpu.VMEM((quads + later, 1, width), F32),
            pltpu.VMEM((n_rows, tokens, LANES), BF16),
            pltpu.VMEM((PATCH * frames, channels, LANES), BF16),
            dma((9,)),
            dma((frames, 2)), dma((frames, 2)),
            dma((frames, rows)), dma((frames, rows)),
            dma((n_rows,)), dma((n_rows,)),
            dma((2 * quads + later + 1,)), dma((2 * quads + later + 1,)),
            dma((quads + later,)), dma((quads + later,)),
            pltpu.SemaphoreType.REGULAR((max(n_rows - 2, 1),)),
        ],
        compiler_params=pltpu.CompilerParams(
            collective_id=0, has_side_effects=True, vmem_limit_bytes=56 * 2**20
        ),
        name="encode",
    )(
        features,
        spatial_weight.reshape(9 * channels, channels),
        temporal_weight.reshape(3 * channels, channels),
        head_weight.T,
        embed_weight,
        part,
        scale,
        shift,
        qkv_weight,
    )
    count = frames * n_rows * tokens
    return pl.pallas_call(
        functools.partial(project, n_rows, frames),
        out_shape=jax.ShapeDtypeStruct((count, width), F32),
        in_specs=[vmem] * 4,
        out_specs=hbm,
        scratch_shapes=[pltpu.VMEM((count, width), F32), dma((4 * frames,))],
        compiler_params=pltpu.CompilerParams(vmem_limit_bytes=32 * 2**20),
        name="project",
    )(block, fold.reshape(pdim, width), shift_row, gram)


def solution(mesh):
    return jax.shard_map(
        functools.partial(per_device, mesh.shape["groups"], mesh.shape["tm"], mesh.shape["rows"]),
        mesh=mesh,
        in_specs=(
            P(("groups", "tm"), "rows", None, None),
            P(),
            P(),
            P(),
            P(),
            P(),
            P(),
            P("tm", "rows"),
        ),
        out_specs=P(("groups", "tm"), "rows"),
        check_vma=False,
    )
```

time: 30.5 us -> 22.8 us (0.75)
  Pallas kernels: 30.2 us -> 22.7 us
    pallas_call x2, Pallas kernels: 30.2 us -> 22.7 us  [the longest x1 20.5 us: per_device(): pl.pallas_call(functools.partial(encode, n_tm, n_rows, split, aligned), o...]
where the time goes in v3:
time: 22.8 us; the launch traced here: 22.7 us
  Pallas kernels  22.7 us (100%)
    pallas_call x1, Pallas kernels, per_device(): pl.pallas_call(functools.partial(encode, n_tm, n_rows, split, aligned), o...  20.5 us
    pallas_call x1, Pallas kernels, per_device(): pl.pallas_call(functools.partial(project, n_rows, frames), out_shape=jax....  2.18 us

profile of v3, /device:TPU:0, one launch (start us, length us, event | category | flops | bytes accessed | tf_op | source)
XLA Modules:
  0.0 22.7 jit_solution(4536003845060613138)
XLA Ops:
  0.0 20.5 %encode.1 = (bf16[4,48,128]{2,1,0:T(8,128)(2,1)S(1)}, bf16[2,4,8,2304]{3,2,1,0:T(8,128)(2,1)S(1)}, f32[1,2304]{1,0:T(1,128)S(1)}, bf16[3,64,64]{2,1,0:T(8,128)(2,1)S(1)}) custom-call(bf16[2,2,96,512]{3,2,1,0:T(8,128)(2,1)} %features.1, bf16[4608,512]{1,0:T(8,128)(2,1)} %bitcast.7, bf16[1536,512]{1,0:T(8,128)(2,1)} %bitcast.8, bf16[16,512]{1,0:T(8,128)(2,1)} %bitcast.9, ...), custom_call_target="tpu_custom_call" | custom-call | tf_op jit(solution)/shard_map/encode/pallas_call | solution.py:472
  20.5 2.2 %project.1 = f32[384,2304]{1,0:T(8,128)} custom-call(bf16[4,48,128]{2,1,0:T(8,128)(2,1)S(1)} %get-tuple-element.9.block, bf16[64,2304]{1,0:T(8,128)(2,1)S(1)} %bitcast.6, f32[1,2304]{1,0:T(1,128)S(1)} %get-tuple-element.11.shift, bf16[3,64,64]{2,1,0:T(8,128)(2,1)S(1)} %get-tuple-element.12.gram), custom_call_target="tpu_custom_call" | custom-call | tf_op jit(solution)/shard_map/project/pallas_call | solution.py:535

commit v4 on v3

v4 whole, which is shorter than its diff:
```python
import functools

import jax
import jax.numpy as jnp
from jax import lax
from jax.experimental import pallas as pl
from jax.experimental.pallas import tpu as pltpu
from jax.sharding import PartitionSpec as P

MESH = pl.DeviceIdType.MESH
PATCH = 2
LANES = 128
EPS = 1e-06
F32 = jnp.float32
BF16 = jnp.bfloat16


def dot(a, b):
    return jnp.dot(a, b, preferred_element_type=F32)


def dot_t(a, b):
    return lax.dot_general(a, b, (((1,), (1,)), ((), ())), preferred_element_type=F32)


def norm_silu(values):
    scaled = values * lax.rsqrt(jnp.mean(values * values, axis=-1, keepdims=True) + EPS)
    half = 0.5 * scaled
    return half + half * jnp.tanh(half)


def encode(
    n_tm, n_rows, split, aligned,
    features, spatial_hbm, temporal_hbm, head_hbm, embed_hbm, part_hbm, scale_hbm, shift_hbm, qkv_hbm,
    block_out, fold_out, shift_out, gram_out,
    feat, halo, taps, spat_w, temp_w, head_w, embed, part, scale_v, shift_v, vectors, wide, qkv_w,
    mixed, side, partial, lat, ahead, part_b, core_in, keep, cross, quad_in, stage, fold, shifts, shifts_in, gathered, heads,
    load_sem, halo_send, halo_recv, next_send, next_recv, mix_send, mix_recv,
    all_send, all_recv, ahead_send, ahead_recv, zero_send,
    fold_send, fold_recv, shift_send, shift_recv, relay, corner,
):
    group, tile, row = lax.axis_index("groups"), lax.axis_index("tm"), lax.axis_index("rows")
    frames, rows, columns, channels = features.shape
    depth, width = qkv_w.shape
    pdim, wide_all = embed.shape
    latent = head_w.shape[0]
    _, quads, block_rows, _ = fold.shape
    has_above, has_below = row > 0, row < n_rows - 1
    has_before, has_after = tile > 0, tile < n_tm - 1
    near = [({"rows": row - 1}, has_above), ({"rows": row + 1}, has_below)]
    count_rows = has_above.astype(jnp.int32) + has_below.astype(jnp.int32)
    count_tiles = has_before.astype(jnp.int32) + has_after.astype(jnp.int32)
    core = lax.rem(tile, 2)
    other_core = {"tm": tile + 1 - 2 * core}

    def flipped(bit):
        return tile + bit * (1 - 2 * lax.rem(tile // bit, 2))

    bits = [("tm", lax.rem(tile // 2, 2), flipped(2))] if n_tm >= 4 else []
    if split:
        bits.append(("groups", group, 1 - group))
    mine = sum((bit[1] * 2**n for n, bit in enumerate(bits)), 0)
    direct = []
    for mask in range(1, quads):
        chosen = [n for n in range(len(bits)) if mask >> n & 1]
        place = mine + sum(2**n * (1 - 2 * bits[n][1]) for n in chosen)
        direct.append(({bits[n][0]: bits[n][2] for n in chosen}, place))
    later = []
    step = 4
    while step < n_tm:
        later.append({"tm": flipped(step)})
        step *= 2
    partners = [other_core] + [device for device, _ in direct if len(device) == 1] + later

    def signal(sem, device):
        pl.semaphore_signal(sem, inc=1, device_id=device, device_id_type=MESH)

    barrier = pltpu.get_barrier_semaphore()
    for device in partners:
        signal(barrier, device)
    for device, there in near + [({"tm": tile - 1}, has_before), ({"tm": tile + 1}, has_after)]:

        @pl.when(there)
        def _():
            signal(barrier, device)

    def load(source, target, index):
        copy = pltpu.make_async_copy(source, target, load_sem.at[index])
        copy.start()
        return copy

    first = group * depth if split else 0
    load_feat = [load(features.at[f], feat.at[frames - f], 9 * f) for f in range(frames)]
    load_embed = load(embed_hbm, embed, 1)
    load_scale = load(scale_hbm, scale_v, 2)
    load_shift = load(shift_hbm, shift_v, 3)
    if not aligned:
        load_part = load(part_hbm, part, 4)
    load_qkv = load(qkv_hbm.at[pl.ds(pl.multiple_of(first, 16), depth)], qkv_w, 5)
    load_spat = load(spatial_hbm, spat_w, 6)
    load_temp = load(temporal_hbm, temp_w, 7)
    load_head = load(head_hbm, head_w, 8)

    def remote(source, target, send, recv, device):
        return pltpu.make_async_remote_copy(
            src_ref=source, dst_ref=target, send_sem=send, recv_sem=recv,
            device_id=device, device_id_type=MESH,
        )

    def up_copy(f):
        return remote(
            features.at[f, 0], halo.at[f, 1], halo_send.at[f, 0], halo_recv.at[f, 1], near[0][0]
        )

    def down_copy(f):
        return remote(
            features.at[f, rows - 1], halo.at[f, 0], halo_send.at[f, 1], halo_recv.at[f, 0], near[1][0]
        )

    next_copy = remote(features.at[0], feat.at[0], next_send.at[0], next_recv.at[0], {"tm": tile - 1})

    def mix_copy(f, r):
        lines = pl.ds(r * columns, columns)
        return remote(
            mixed.at[f, lines], side.at[1 - f, lines], mix_send.at[f, r], mix_recv.at[1 - f, r],
            {"tm": tile - 1 + 2 * f},
        )

    order = (core, 1 - core)
    forward = (core == 1, core == 0)
    neighboured = [
        jnp.logical_or(jnp.logical_and(up, has_after), jnp.logical_and(jnp.logical_not(up), has_before))
        for up in forward
    ]
    pl.semaphore_wait(barrier, len(partners) + count_rows + count_tiles)
    for f in order:
        @pl.when(has_above)
        def _():
            up_copy(f).start()

        @pl.when(has_below)
        def _():
            down_copy(f).start()

    @pl.when(has_before)
    def _():
        next_copy.start()

    phases = n_rows - 1
    done_phases = [0]

    def tell(phase):
        if phase < phases:
            for device, there in near:

                @pl.when(there)
                def _():
                    signal(relay.at[phase], device)

    def next_phase():
        phase = done_phases[0]
        if phase < phases:
            pl.semaphore_wait(relay.at[phase], count_rows)
            tell(phase + 1)
            done_phases[0] = phase + 1

    tell(0)
    if len(bits) == 2:
        signal(corner.at[0], {bits[1][0]: bits[1][2]})

    @pl.when(jnp.logical_not(has_above))
    def _():
        for f in range(frames):
            halo[f, 0] = jnp.zeros(halo.shape[2:], BF16)

    @pl.when(jnp.logical_not(has_below))
    def _():
        for f in range(frames):
            halo[f, 1] = jnp.zeros(halo.shape[2:], BF16)

    @pl.when(jnp.logical_not(has_before))
    def _():
        side[0] = jnp.zeros(side.shape[1:], BF16)

    @pl.when(jnp.logical_not(has_after))
    def _():
        side[1] = jnp.zeros(side.shape[1:], BF16)
        feat[0] = jnp.zeros(feat.shape[1:], BF16)

    span = 3 * channels
    column = lax.broadcasted_iota(jnp.int32, (columns, channels), 0)

    def spread_taps(values, place, frame):
        active = norm_silu(values.astype(F32))
        left = jnp.where(column == 0, 0.0, pltpu.roll(active, 1, 0))
        right = jnp.where(column == columns - 1, 0.0, pltpu.roll(active, columns - 1, 0))
        for k, shifted in enumerate((left, active, right)):
            taps[frame, :, pl.ds(place * span + k * channels, channels)] = shifted.astype(BF16)

    load_embed.wait()
    load_scale.wait()
    load_shift.wait()
    mean = jnp.mean(embed[...].astype(F32), axis=1, keepdims=True)
    if aligned:
        start = pl.multiple_of(tile * (wide_all // n_tm) + first, LANES)
        own = embed[:, pl.ds(start, depth)].astype(F32)
        vectors[0] = scale_v[...].astype(F32)
        vectors[1] = shift_v[...].astype(F32)
        at = start // LANES
        scale, shift = (
            jnp.concatenate([vectors[v, pl.ds(at + j, 1)] for j in range(depth // LANES)], axis=1)
            for v in range(2)
        )
    else:
        load_part.wait()
        own, scale, shift = part[...].astype(F32), scale_v[...].astype(F32), shift_v[...].astype(F32)
    scaled = ((own - mean) * (1.0 + scale)).astype(BF16)
    rows16 = lax.broadcasted_iota(jnp.int32, (16, depth), 0)
    shift16 = jnp.where(rows16 == 0, jnp.broadcast_to(shift, (16, depth)), 0.0).astype(BF16)
    lhs = jnp.concatenate([scaled, shift16], axis=0)
    load_qkv.wait()
    chunk = width // 3
    for n in range(3):
        cols = pl.ds(n * chunk, chunk)
        terms = dot(lhs, qkv_w[:, cols])
        shifts[0, :, cols] = terms[pdim : pdim + 1]
        for c in range(2):
            for b in range(quads):
                low = (c * quads + b) * block_rows
                piece = terms[low : low + block_rows]
                keep[c, b, :, cols] = piece
                part_b[c, b, :, cols] = piece.astype(BF16)

    core_copies = [
        remote(part_b.at[1 - core], core_in, fold_send.at[0], fold_recv.at[0], other_core),
        remote(shifts.at[0], shifts_in.at[0], shift_send.at[0], shift_recv.at[0], other_core),
    ]
    for copy in core_copies:
        copy.start()

    for copy in load_feat:
        copy.wait()
    for f in range(frames):
        for r in range(rows):
            spread_taps(feat[frames - f, r], r + 1, f)
    load_spat.wait()
    inner = taps[:, :, span : 3 * span].reshape(frames * columns, 2 * span)
    direct_copies = []
    for r in range(rows):
        total = dot(inner, spat_w[(1 - r) * span : (3 - r) * span])
        for f in range(frames):
            partial[f, pl.ds(r * columns, columns)] = total[f * columns : (f + 1) * columns]
        if r == 0:
            for copy in core_copies:
                copy.wait()
            shifts[1] = shifts[0] + shifts_in[0]
            for b in range(quads):
                cross[b] = (keep[core, b] + core_in[b].astype(F32)).astype(BF16)
            for m, (device, place) in enumerate(direct, 1):
                direct_copies += [
                    remote(cross.at[place], quad_in.at[m], fold_send.at[m], fold_recv.at[m], device),
                    remote(shifts.at[1], shifts_in.at[m], shift_send.at[m], shift_recv.at[m], device),
                ]
            if len(bits) == 2:
                pl.semaphore_wait(corner.at[0], 1)
            for copy in direct_copies:
                copy.start()
    next_phase()

    def end_direct():
        total = keep[core, mine] + core_in[mine].astype(F32)
        shift_total = shifts[1]
        for copy in direct_copies:
            copy.wait()
        for m in range(1, quads):
            total = total + quad_in[m].astype(F32)
            shift_total = shift_total + shifts_in[m]
        for n, device in enumerate(later):
            stage[2 * n] = total.astype(BF16)
            shifts[2 + n] = shift_total
            pair_copies = [
                remote(
                    stage.at[2 * n], stage.at[2 * n + 1],
                    fold_send.at[quads + n], fold_recv.at[quads + n], device,
                ),
                remote(
                    shifts.at[2 + n], shifts_in.at[quads + n],
                    shift_send.at[quads + n], shift_recv.at[quads + n], device,
                ),
            ]
            for copy in pair_copies:
                copy.start()
            for copy in pair_copies:
                copy.wait()
            total = total + stage[2 * n + 1].astype(F32)
            shift_total = shift_total + shifts_in[quads + n]
        fold[core, mine] = total.astype(BF16)
        shift_out[...] = shift_total
        for copy in share_copies:
            copy.start()

    base = quads + len(later)
    share_copies = [
        remote(
            fold.at[core, mine], fold.at[core, mine], fold_send.at[base + m], fold_recv.at[base + m], device
        )
        for m, (device, _) in enumerate(direct)
    ]
    base += len(share_copies)

    load_head.wait()

    def place_heads():
        lane = lax.broadcasted_iota(jnp.int32, (latent, LANES), 1)
        latent_lane = lax.broadcasted_iota(jnp.int32, (latent, LANES), 0)
        pair = PATCH * latent
        for a in range(PATCH):
            low = a * pair
            pick = (lane >= low) & (lane < low + pair) & (lax.rem(lane, latent) == latent_lane)
            spread_head = lax.dot_general(
                head_w[...], jnp.where(pick, 1.0, 0.0).astype(BF16), (((0,), (0,)), ((), ())),
                preferred_element_type=F32,
            )
            heads[a] = spread_head.astype(BF16)

    def finish_frame(f, there):
        @pl.when(has_above)
        def _():
            down_copy(f).wait_recv()

        @pl.when(has_below)
        def _():
            up_copy(f).wait_recv()

        spread_taps(halo[f, 0], 0, f)
        spread_taps(halo[f, 1], rows + 1, f)
        for r, (place, weights) in enumerate(
            ((0, spat_w[0:span]), (3 * span, spat_w[2 * span : 3 * span]))
        ):
            lines = pl.ds(r * columns, columns)
            total = partial[f, lines] + dot(taps[f, :, pl.ds(place, span)], weights)
            mixed[f, lines] = norm_silu(total).astype(BF16)

            @pl.when(there)
            def _():
                mix_copy(f, r).start()

    @pl.when(core == 0)
    def _():
        place_heads()

    finish_frame(order[0], neighboured[0])
    next_phase()
    finish_frame(order[1], neighboured[1])

    @pl.when(core == 1)
    def _():
        place_heads()

    load_temp.wait()
    own_frames = jnp.concatenate([mixed[0], mixed[1]], axis=1)
    partial[0] = dot(own_frames, temp_w[0:2].reshape(2 * channels, channels))
    partial[1] = dot(own_frames, temp_w[1:3].reshape(2 * channels, channels))

    end_direct()

    while done_phases[0] < phases:
        next_phase()

    @pl.when(has_after)
    def _():
        next_copy.wait_recv()

    tokens = columns // PATCH
    out_lane = lax.broadcasted_iota(jnp.int32, (tokens, LANES), 1)
    even_lane = lax.rem(out_lane // latent, PATCH) == 0

    def patches_of(total, residual):
        total = total + jnp.concatenate([feat[residual, r].astype(F32) for r in range(rows)], axis=0)
        active = norm_silu(total).astype(BF16)
        lat[...] = dot(active[:columns], heads[0]) + dot(active[columns:], heads[1])
        even = lat[pl.ds(0, tokens, stride=PATCH), :]
        odd = lat[pl.ds(1, tokens, stride=PATCH), :]
        return jnp.where(even_lane, even, odd).astype(BF16)

    def away(d):
        return lax.rem(row + d, n_rows)

    sends = [
        remote(
            gathered.at[1, row], gathered.at[1, row], all_send.at[d], all_recv.at[d], {"rows": away(d)}
        )
        for d in range(1, n_rows)
    ]
    ahead_sends = [
        remote(
            ahead, gathered.at[0, row], ahead_send.at[d], ahead_recv.at[d],
            {"tm": tile + 1, "rows": away(d)},
        )
        for d in range(n_rows)
    ]
    zero_sends = [
        remote(
            gathered.at[0, row], gathered.at[0, row], zero_send.at[d], ahead_recv.at[d], {"rows": away(d)}
        )
        for d in range(1, n_rows)
    ]

    is_first = tile == 0

    @pl.when(is_first)
    def _():
        gathered[0, row] = patches_of(dot(mixed[0], temp_w[2]), frames)
        for copy in zero_sends:
            copy.start()

    slots = jnp.where(is_first, 1, core)
    for s, own in ((slots, slots == 1), (1 - slots, slots == 0)):
        filled = jnp.logical_or(
            jnp.logical_and(own, has_before), jnp.logical_and(jnp.logical_not(own), has_after)
        )

        @pl.when(filled)
        def _():
            for r in range(rows):
                mix_copy(s, r).wait_recv()

        patches = patches_of(partial[s] + dot(side[1 - s], temp_w[2 * (1 - s)]), s)

        @pl.when(own)
        def _():
            gathered[1, row] = patches
            for copy in sends:
                copy.start()

        @pl.when(jnp.logical_and(jnp.logical_not(own), has_after))
        def _():
            ahead[...] = patches
            for copy in ahead_sends:
                copy.start()

    for copy in share_copies:
        copy.wait()
    widen = remote(fold.at[core], fold.at[core], fold_send.at[base], fold_recv.at[base], other_core)
    widen.start()

    centred = embed[...].astype(F32) - mean
    high = centred.astype(BF16)
    wide[0:pdim] = high
    wide[pdim:] = (centred - high.astype(F32)).astype(BF16)
    products = dot_t(wide[...], wide[...])
    gram = (
        products[:pdim, :pdim] + products[:pdim, pdim:]
        + products[pdim:, :pdim] + products[pdim:, pdim:]
    ) * (1.0 / wide_all)
    for i in range(3):
        piece = gram.astype(BF16)
        gram_out[i] = piece
        gram = gram - piece.astype(F32)

    @pl.when(has_above)
    def _():
        for f in range(frames):
            up_copy(f).wait_send()

    @pl.when(has_below)
    def _():
        for f in range(frames):
            down_copy(f).wait_send()

    @pl.when(has_before)
    def _():
        next_copy.wait_send()
        for r in range(rows):
            mix_copy(0, r).wait_send()

    @pl.when(has_after)
    def _():
        for r in range(rows):
            mix_copy(1, r).wait_send()
        for copy in ahead_sends:
            copy.wait_send()

    @pl.when(is_first)
    def _():
        for copy in zero_sends:
            copy.wait_send()

    widen.wait()
    fold_out[...] = fold[...]
    for copy in sends:
        copy.wait()

    @pl.when(has_before)
    def _():
        ahead_sends[0].wait_recv()

    for copy in ahead_sends[1:]:
        copy.wait_recv()
    block_out[...] = gathered[...]


def project(block, fold, shift, gram, out, held, sems):
    pdim, width = fold.shape
    frames, n_rows, tokens, _ = block.shape
    parts = 4
    lines = n_rows * tokens // parts
    copies = []
    for f in range(frames):
        patches = block[f].reshape(n_rows * tokens, LANES)[:, :pdim]
        for n in range(parts):
            own = patches[n * lines : (n + 1) * lines]
            moved = dot(own, gram[0]) + dot(own, gram[1]) + dot(own, gram[2])
            spread = jnp.maximum(jnp.sum(moved * own.astype(F32), axis=-1, keepdims=True), 0.0)
            here = pl.ds((f * parts + n) * lines, lines)
            held[here] = dot(own, fold[...]) * lax.rsqrt(spread + EPS) + shift[...]
            copy = pltpu.make_async_copy(held.at[here], out.at[here], sems.at[f * parts + n])
            copy.start()
            copies.append(copy)
    for copy in copies:
        copy.wait()


def per_device(
    n_groups, n_tm, n_rows,
    features, spatial_weight, temporal_weight, head_weight, embed_weight, ada_scale, ada_shift, qkv_weight,
):
    frames, rows, columns, channels = features.shape
    depth, width = qkv_weight.shape
    pdim, wide_all = embed_weight.shape
    latent = head_weight.shape[1]
    split = n_groups == 2
    depth = depth // 2 if split else depth
    aligned = depth % LANES == 0
    quads = (2 if split else 1) * (2 if n_tm >= 4 else 1)
    later = max(n_tm.bit_length() - 3, 0)
    block_rows = pdim // (2 * quads)
    fold_shape = (2, quads, block_rows, width)
    part = embed_weight
    scale, shift = (v.reshape(wide_all // LANES, LANES) for v in (ada_scale, ada_shift))
    if not aligned:
        scale, shift = ada_scale[None], ada_shift[None]
        start = lax.axis_index("tm") * qkv_weight.shape[0]
        if split:
            start = start + lax.axis_index("groups") * depth
        scale, shift, part = (lax.dynamic_slice_in_dim(v, start, depth, axis=1) for v in (scale, shift, part))
    hbm = pl.BlockSpec(memory_space=pl.ANY)
    vmem = pl.BlockSpec(memory_space=pltpu.VMEM)
    tokens = columns // PATCH
    dma = pltpu.SemaphoreType.DMA
    block, fold, shift_row, gram = pl.pallas_call(
        functools.partial(encode, n_tm, n_rows, split, aligned),
        out_shape=(
            pltpu.VMEM((frames, n_rows, tokens, LANES), BF16),
            pltpu.VMEM(fold_shape, BF16),
            pltpu.VMEM((1, width), F32),
            pltpu.VMEM((3, pdim, pdim), BF16),
        ),
        in_specs=[hbm] * 9,
        out_specs=(vmem, vmem, vmem, vmem),
        scratch_shapes=[
            pltpu.VMEM((frames + 1, rows, columns, channels), BF16),
            pltpu.VMEM((frames, 2, columns, channels), BF16),
            pltpu.VMEM((frames, columns, (rows + 2) * 3 * channels), BF16),
            pltpu.VMEM((9 * channels, channels), BF16),
            pltpu.VMEM((3, channels, channels), BF16),
            pltpu.VMEM((latent, channels), BF16),
            pltpu.VMEM((pdim, wide_all), BF16),
            pltpu.VMEM((pdim, depth), BF16),
            pltpu.VMEM(scale.shape, BF16),
            pltpu.VMEM(shift.shape, BF16),
            pltpu.VMEM((2, wide_all // LANES, LANES), F32),
            pltpu.VMEM((2 * pdim, wide_all), BF16),
            pltpu.VMEM((depth, width), BF16),
            pltpu.VMEM((frames, rows * columns, channels), BF16),
            pltpu.VMEM((frames, rows * columns, channels), BF16),
            pltpu.VMEM((frames, rows * columns, channels), F32),
            pltpu.VMEM((columns, LANES), F32),
            pltpu.VMEM((tokens, LANES), BF16),
            pltpu.VMEM(fold_shape, BF16),
            pltpu.VMEM(fold_shape[1:], BF16),
            pltpu.VMEM(fold_shape, F32),
            pltpu.VMEM(fold_shape[1:], BF16),
            pltpu.VMEM(fold_shape[1:], BF16),
            pltpu.VMEM((max(2 * later, 1), block_rows, width), BF16),
            pltpu.VMEM(fold_shape, BF16),
            pltpu.VMEM((2 + later, 1, width), F32),
            pltpu.VMEM((quads + later, 1, width), F32),
            pltpu.VMEM((frames, n_rows, tokens, LANES), BF16),
            pltpu.VMEM((PATCH, channels, LANES), BF16),
            dma((10,)),
            dma((frames, 2)), dma((frames, 2)),
            dma((1,)), dma((1,)),
            dma((frames, rows)), dma((frames, rows)),
            dma((n_rows,)), dma((n_rows,)),
            dma((n_rows,)), dma((n_rows,)), dma((n_rows,)),
            dma((2 * quads + later + 1,)), dma((2 * quads + later + 1,)),
            dma((quads + later,)), dma((quads + later,)),
            pltpu.SemaphoreType.REGULAR((max(n_rows - 1, 1),)),
            pltpu.SemaphoreType.REGULAR((1,)),
        ],
        compiler_params=pltpu.CompilerParams(
            collective_id=0, has_side_effects=True, vmem_limit_bytes=56 * 2**20
        ),
        name="encode",
    )(
        features,
        spatial_weight.reshape(9 * channels, channels),
        temporal_weight,
        head_weight.T,
        embed_weight,
        part,
        scale,
        shift,
        qkv_weight,
    )
    count = frames * n_rows * tokens
    return pl.pallas_call(
        project,
        out_shape=jax.ShapeDtypeStruct((count, width), F32),
        in_specs=[vmem] * 4,
        out_specs=hbm,
        scratch_shapes=[pltpu.VMEM((count, width), F32), dma((4 * frames,))],
        compiler_params=pltpu.CompilerParams(vmem_limit_bytes=32 * 2**20),
        name="project",
    )(block, fold.reshape(pdim, width), shift_row, gram)


def solution(mesh):
    return jax.shard_map(
        functools.partial(per_device, mesh.shape["groups"], mesh.shape["tm"], mesh.shape["rows"]),
        mesh=mesh,
        in_specs=(
            P(("groups", "tm"), "rows", None, None),
            P(),
            P(),
            P(),
            P(),
            P(),
            P(),
            P("tm", "rows"),
        ),
        out_specs=P(("groups", "tm"), "rows"),
        check_vma=False,
    )
```

time: 22.8 us -> 21.2 us (0.930)
  the two profiles are of different devices: /device:TPU:0 before, /device:TPU:6 now
where the time goes in v4:
time: 21.2 us; the launch traced here: 21 us
  Pallas kernels  21 us (99%)
    pallas_call x1, Pallas kernels, per_device(): pl.pallas_call(functools.partial(encode, n_tm, n_rows, split, aligned), o...  18.9 us
    pallas_call x1, Pallas kernels, per_device(): pl.pallas_call(project, out_shape=jax.ShapeDtypeStruct((count, width), F3...  2.16 us

profile of v4, /device:TPU:6, one launch (start us, length us, event | category | flops | bytes accessed | tf_op | source)
XLA Modules:
  0.0 21.0 jit_solution(18365730152514150166)
XLA Ops:
  0.0 18.9 %encode.1 = (bf16[2,4,48,128]{3,2,1,0:T(8,128)(2,1)S(1)}, bf16[2,4,8,2304]{3,2,1,0:T(8,128)(2,1)S(1)}, f32[1,2304]{1,0:T(1,128)S(1)}, bf16[3,64,64]{2,1,0:T(8,128)(2,1)S(1)}) custom-call(bf16[2,2,96,512]{3,2,1,0:T(8,128)(2,1)} %features.1, bf16[4608,512]{1,0:T(8,128)(2,1)} %bitcast.6, bf16[3,512,512]{2,1,0:T(8,128)(2,1)} %temporal_hbm.1, ...), custom_call_target="tpu_custom_call" | custom-call | tf_op jit(solution)/shard_map/encode/pallas_call | solution.py:551
  18.9 2.2 %project.1 = f32[384,2304]{1,0:T(8,128)} custom-call(bf16[2,4,48,128]{3,2,1,0:T(8,128)(2,1)S(1)} %get-tuple-element.9.block, bf16[64,2304]{1,0:T(8,128)(2,1)S(1)} %bitcast.5, f32[1,2304]{1,0:T(1,128)S(1)} %get-tuple-element.11.shift, bf16[3,64,64]{2,1,0:T(8,128)(2,1)S(1)} %get-tuple-element.12.gram), custom_call_target="tpu_custom_call" | custom-call | tf_op jit(solution)/shard_map/project/pallas_call | solution.py:618

commit v5 on v4

--- a/solution.py
+++ b/solution.py
@@ -34,8 +34,8 @@
     features, spatial_hbm, temporal_hbm, head_hbm, embed_hbm, part_hbm, scale_hbm, shift_hbm, qkv_hbm,
     block_out, fold_out, shift_out, gram_out,
     feat, halo, taps, spat_w, temp_w, head_w, embed, part, scale_v, shift_v, vectors, wide, qkv_w,
-    mixed, side, partial, lat, ahead, part_b, core_in, keep, cross, quad_in, stage, fold, shifts, shifts_in, gathered, heads,
-    load_sem, halo_send, halo_recv, next_send, next_recv, mix_send, mix_recv,
+    mixed, side, bracket, partial, lat, ahead, part_b, core_in, keep, cross, quad_in, stage, fold, shifts, shifts_in, gathered, heads,
+    load_sem, halo_send, halo_recv, mix_send, mix_recv,
     all_send, all_recv, ahead_send, ahead_recv, zero_send,
     fold_send, fold_recv, shift_send, shift_recv, relay, corner,
 ):
@@ -90,16 +90,20 @@
         return copy
 
     first = group * depth if split else 0
-    load_feat = [load(features.at[f], feat.at[frames - f], 9 * f) for f in range(frames)]
+    load_feat = load(features, feat, 0)
     load_embed = load(embed_hbm, embed, 1)
     load_scale = load(scale_hbm, scale_v, 2)
     load_shift = load(shift_hbm, shift_v, 3)
     if not aligned:
-        load_part = load(part_hbm, part, 4)
-    load_qkv = load(qkv_hbm.at[pl.ds(pl.multiple_of(first, 16), depth)], qkv_w, 5)
-    load_spat = load(spatial_hbm, spat_w, 6)
-    load_temp = load(temporal_hbm, temp_w, 7)
-    load_head = load(head_hbm, head_w, 8)
+        load_part = load(part_hbm, part, 9)
+    load_qkv = load(qkv_hbm.at[pl.ds(pl.multiple_of(first, 16), depth)], qkv_w, 4)
+    span = 3 * channels
+    load_spat = [
+        load(spatial_hbm.at[lines], spat_w.at[lines], index)
+        for lines, index in ((pl.ds(span, 2 * span), 5), (pl.ds(0, span), 8))
+    ]
+    load_temp = load(temporal_hbm, temp_w, 6)
+    load_head = load(head_hbm, head_w, 7)
 
     def remote(source, target, send, recv, device):
         return pltpu.make_async_remote_copy(
@@ -109,29 +113,18 @@
 
     def up_copy(f):
         return remote(
-            features.at[f, 0], halo.at[f, 1], halo_send.at[f, 0], halo_recv.at[f, 1], near[0][0]
+            features.at[f, 0], halo.at[f, 1], halo_send.at[0], halo_recv.at[f, 1], near[0][0]
         )
 
     def down_copy(f):
         return remote(
-            features.at[f, rows - 1], halo.at[f, 0], halo_send.at[f, 1], halo_recv.at[f, 0], near[1][0]
+            features.at[f, rows - 1], halo.at[f, 0], halo_send.at[1], halo_recv.at[f, 0], near[1][0]
         )
 
-    next_copy = remote(features.at[0], feat.at[0], next_send.at[0], next_recv.at[0], {"tm": tile - 1})
-
-    def mix_copy(f, r):
-        lines = pl.ds(r * columns, columns)
-        return remote(
-            mixed.at[f, lines], side.at[1 - f, lines], mix_send.at[f, r], mix_recv.at[1 - f, r],
-            {"tm": tile - 1 + 2 * f},
-        )
+    onward = remote(mixed.at[1], side.at[0], mix_send.at[1], mix_recv.at[0], {"tm": tile + 1})
+    back = remote(bracket, side.at[1], mix_send.at[0], mix_recv.at[1], {"tm": tile - 1})
 
     order = (core, 1 - core)
-    forward = (core == 1, core == 0)
-    neighboured = [
-        jnp.logical_or(jnp.logical_and(up, has_after), jnp.logical_and(jnp.logical_not(up), has_before))
-        for up in forward
-    ]
     pl.semaphore_wait(barrier, len(partners) + count_rows + count_tiles)
     for f in order:
         @pl.when(has_above)
@@ -141,10 +134,6 @@
         @pl.when(has_below)
         def _():
             down_copy(f).start()
-
-    @pl.when(has_before)
-    def _():
-        next_copy.start()
 
     phases = n_rows - 1
     done_phases = [0]
@@ -182,12 +171,6 @@
     def _():
         side[0] = jnp.zeros(side.shape[1:], BF16)
 
-    @pl.when(jnp.logical_not(has_after))
-    def _():
-        side[1] = jnp.zeros(side.shape[1:], BF16)
-        feat[0] = jnp.zeros(feat.shape[1:], BF16)
-
-    span = 3 * channels
     column = lax.broadcasted_iota(jnp.int32, (columns, channels), 0)
 
     def spread_taps(values, place, frame):
@@ -196,6 +179,11 @@
         right = jnp.where(column == columns - 1, 0.0, pltpu.roll(active, columns - 1, 0))
         for k, shifted in enumerate((left, active, right)):
             taps[frame, :, pl.ds(place * span + k * channels, channels)] = shifted.astype(BF16)
+
+    load_feat.wait()
+    for f in range(frames):
+        for r in range(rows):
+            spread_taps(feat[f, r], r + 1, f)
 
     load_embed.wait()
     load_scale.wait()
@@ -214,16 +202,19 @@
     else:
         load_part.wait()
         own, scale, shift = part[...].astype(F32), scale_v[...].astype(F32), shift_v[...].astype(F32)
-    scaled = ((own - mean) * (1.0 + scale)).astype(BF16)
+    scaled = (own - mean) * (1.0 + scale)
+    upper = scaled.astype(BF16)
+    lower = (scaled - upper.astype(F32)).astype(BF16)
     rows16 = lax.broadcasted_iota(jnp.int32, (16, depth), 0)
     shift16 = jnp.where(rows16 == 0, jnp.broadcast_to(shift, (16, depth)), 0.0).astype(BF16)
-    lhs = jnp.concatenate([scaled, shift16], axis=0)
+    lhs = jnp.concatenate([upper, lower, shift16], axis=0)
     load_qkv.wait()
     chunk = width // 3
     for n in range(3):
         cols = pl.ds(n * chunk, chunk)
         terms = dot(lhs, qkv_w[:, cols])
-        shifts[0, :, cols] = terms[pdim : pdim + 1]
+        shifts[0, :, cols] = terms[2 * pdim : 2 * pdim + 1]
+        terms = terms[:pdim] + terms[pdim : 2 * pdim]
         for c in range(2):
             for b in range(quads):
                 low = (c * quads + b) * block_rows
@@ -238,15 +229,10 @@
     for copy in core_copies:
         copy.start()
 
-    for copy in load_feat:
-        copy.wait()
-    for f in range(frames):
-        for r in range(rows):
-            spread_taps(feat[frames - f, r], r + 1, f)
-    load_spat.wait()
     inner = taps[:, :, span : 3 * span].reshape(frames * columns, 2 * span)
     direct_copies = []
     for r in range(rows):
+        load_spat[r].wait()
         total = dot(inner, spat_w[(1 - r) * span : (3 - r) * span])
         for f in range(frames):
             partial[f, pl.ds(r * columns, columns)] = total[f * columns : (f + 1) * columns]
@@ -258,8 +244,8 @@
                 cross[b] = (keep[core, b] + core_in[b].astype(F32)).astype(BF16)
             for m, (device, place) in enumerate(direct, 1):
                 direct_copies += [
-                    remote(cross.at[place], quad_in.at[m], fold_send.at[m], fold_recv.at[m], device),
-                    remote(shifts.at[1], shifts_in.at[m], shift_send.at[m], shift_recv.at[m], device),
+                    remote(cross.at[place], quad_in.at[m], fold_send.at[1], fold_recv.at[1], device),
+                    remote(shifts.at[1], shifts_in.at[m], shift_send.at[1], shift_recv.at[1], device),
                 ]
             if len(bits) == 2:
                 pl.semaphore_wait(corner.at[0], 1)
@@ -270,8 +256,15 @@
     def end_direct():
         total = keep[core, mine] + core_in[mine].astype(F32)
         shift_total = shifts[1]
-        for copy in direct_copies:
-            copy.wait()
+        if direct:
+            device = direct[0][0]
+            for copy in (
+                remote(quad_in.at[1:], quad_in.at[1:], fold_send.at[1], fold_recv.at[1], device),
+                remote(
+                    shifts_in.at[1:quads], shifts_in.at[1:quads], shift_send.at[1], shift_recv.at[1], device
+                ),
+            ):
+                copy.wait()
         for m in range(1, quads):
             total = total + quad_in[m].astype(F32)
             shift_total = shift_total + shifts_in[m]
@@ -281,11 +274,11 @@
             pair_copies = [
                 remote(
                     stage.at[2 * n], stage.at[2 * n + 1],
-                    fold_send.at[quads + n], fold_recv.at[quads + n], device,
+                    fold_send.at[2 + n], fold_recv.at[2 + n], device,
                 ),
                 remote(
                     shifts.at[2 + n], shifts_in.at[quads + n],
-                    shift_send.at[quads + n], shift_recv.at[quads + n], device,
+                    shift_send.at[2 + n], shift_recv.at[2 + n], device,
                 ),
             ]
             for copy in pair_copies:
@@ -299,14 +292,11 @@
         for copy in share_copies:
             copy.start()
 
-    base = quads + len(later)
+    base = 2 + len(later)
     share_copies = [
-        remote(
-            fold.at[core, mine], fold.at[core, mine], fold_send.at[base + m], fold_recv.at[base + m], device
-        )
-        for m, (device, _) in enumerate(direct)
+        remote(fold.at[core, mine], fold.at[core, mine], fold_send.at[base], fold_recv.at[base], device)
+        for device, _ in direct
     ]
-    base += len(share_copies)
 
     load_head.wait()
 
@@ -323,7 +313,9 @@
             )
             heads[a] = spread_head.astype(BF16)
 
-    def finish_frame(f, there):
+    load_temp.wait()
+
+    def finish_frame(f):
         @pl.when(has_above)
         def _():
             down_copy(f).wait_recv()
@@ -334,49 +326,57 @@
 
         spread_taps(halo[f, 0], 0, f)
         spread_taps(halo[f, 1], rows + 1, f)
+        totals = []
         for r, (place, weights) in enumerate(
             ((0, spat_w[0:span]), (3 * span, spat_w[2 * span : 3 * span]))
         ):
             lines = pl.ds(r * columns, columns)
-            total = partial[f, lines] + dot(taps[f, :, pl.ds(place, span)], weights)
-            mixed[f, lines] = norm_silu(total).astype(BF16)
-
-            @pl.when(there)
+            totals.append(partial[f, lines] + dot(taps[f, :, pl.ds(place, span)], weights))
+        mixed[f] = norm_silu(jnp.concatenate(totals, axis=0)).astype(BF16)
+
+        @pl.when(jnp.logical_and(f == 1, has_after))
+        def _():
+            onward.start()
+
+        @pl.when(f == 0)
+        def _():
+            residual = jnp.concatenate([feat[0, r].astype(F32) for r in range(rows)], axis=0)
+            bracket[...] = (dot(mixed[0], temp_w[2]) + residual).astype(BF16)
+
+            @pl.when(has_before)
             def _():
-                mix_copy(f, r).start()
+                back.start()
 
     @pl.when(core == 0)
     def _():
         place_heads()
 
-    finish_frame(order[0], neighboured[0])
+    finish_frame(order[0])
     next_phase()
-    finish_frame(order[1], neighboured[1])
+    finish_frame(order[1])
 
     @pl.when(core == 1)
     def _():
         place_heads()
 
-    load_temp.wait()
     own_frames = jnp.concatenate([mixed[0], mixed[1]], axis=1)
     partial[0] = dot(own_frames, temp_w[0:2].reshape(2 * channels, channels))
     partial[1] = dot(own_frames, temp_w[1:3].reshape(2 * channels, channels))
 
-    end_direct()
+    early = 2 * row < n_rows
+
+    @pl.when(early)
+    def _():
+        end_direct()
 
     while done_phases[0] < phases:
         next_phase()
-
-    @pl.when(has_after)
-    def _():
-        next_copy.wait_recv()
 
     tokens = columns // PATCH
     out_lane = lax.broadcasted_iota(jnp.int32, (tokens, LANES), 1)
     even_lane = lax.rem(out_lane // latent, PATCH) == 0
 
-    def patches_of(total, residual):
-        total = total + jnp.concatenate([feat[residual, r].astype(F32) for r in range(rows)], axis=0)
+    def patches_of(total):
         active = norm_silu(total).astype(BF16)
         lat[...] = dot(active[:columns], heads[0]) + dot(active[columns:], heads[1])
         even = lat[pl.ds(0, tokens, stride=PATCH), :]
@@ -388,20 +388,20 @@
 
     sends = [
         remote(
-            gathered.at[1, row], gathered.at[1, row], all_send.at[d], all_recv.at[d], {"rows": away(d)}
+            gathered.at[1, row], gathered.at[1, row], all_send.at[0], all_recv.at[0], {"rows": away(d)}
         )
         for d in range(1, n_rows)
     ]
     ahead_sends = [
         remote(
-            ahead, gathered.at[0, row], ahead_send.at[d], ahead_recv.at[d],
+            ahead, gathered.at[0, row], ahead_send.at[0], ahead_recv.at[0],
             {"tm": tile + 1, "rows": away(d)},
         )
         for d in range(n_rows)
     ]
     zero_sends = [
         remote(
-            gathered.at[0, row], gathered.at[0, row], zero_send.at[d], ahead_recv.at[d], {"rows": away(d)}
+            gathered.at[0, row], gathered.at[0, row], zero_send.at[0], ahead_recv.at[0], {"rows": away(d)}
         )
         for d in range(1, n_rows)
     ]
@@ -410,37 +410,50 @@
 
     @pl.when(is_first)
     def _():
-        gathered[0, row] = patches_of(dot(mixed[0], temp_w[2]), frames)
+        gathered[0, row] = patches_of(bracket[...].astype(F32))
         for copy in zero_sends:
             copy.start()
 
-    slots = jnp.where(is_first, 1, core)
-    for s, own in ((slots, slots == 1), (1 - slots, slots == 0)):
-        filled = jnp.logical_or(
-            jnp.logical_and(own, has_before), jnp.logical_and(jnp.logical_not(own), has_after)
-        )
-
-        @pl.when(filled)
-        def _():
-            for r in range(rows):
-                mix_copy(s, r).wait_recv()
-
-        patches = patches_of(partial[s] + dot(side[1 - s], temp_w[2 * (1 - s)]), s)
-
-        @pl.when(own)
-        def _():
-            gathered[1, row] = patches
-            for copy in sends:
-                copy.start()
-
-        @pl.when(jnp.logical_and(jnp.logical_not(own), has_after))
-        def _():
-            ahead[...] = patches
-            for copy in ahead_sends:
-                copy.start()
-
-    for copy in share_copies:
-        copy.wait()
+    def last_frame():
+        @pl.when(has_before)
+        def _():
+            onward.wait_recv()
+
+        residual = jnp.concatenate([feat[1, r].astype(F32) for r in range(rows)], axis=0)
+        gathered[1, row] = patches_of(partial[1] + dot(side[0], temp_w[0]) + residual)
+        for copy in sends:
+            copy.start()
+
+    last_first = jnp.logical_or(is_first, core == 1)
+    late = jnp.logical_not(early)
+
+    @pl.when(last_first)
+    def _():
+        last_frame()
+
+    @pl.when(jnp.logical_and(last_first, late))
+    def _():
+        end_direct()
+
+    @pl.when(has_after)
+    def _():
+        back.wait_recv()
+        ahead[...] = patches_of(partial[0] + side[1].astype(F32))
+        for copy in ahead_sends:
+            copy.start()
+
+    @pl.when(jnp.logical_and(jnp.logical_not(last_first), late))
+    def _():
+        end_direct()
+
+    @pl.when(jnp.logical_not(last_first))
+    def _():
+        last_frame()
+
+    if direct:
+        others = fold.at[core, 0 : quads - 1]
+        remote(others, others, fold_send.at[base], fold_recv.at[base], direct[0][0]).wait()
+    base += 1
     widen = remote(fold.at[core], fold.at[core], fold_send.at[base], fold_recv.at[base], other_core)
     widen.start()
 
@@ -460,43 +473,46 @@
 
     @pl.when(has_above)
     def _():
-        for f in range(frames):
-            up_copy(f).wait_send()
+        edge = features.at[:, 0]
+        remote(edge, halo.at[:, 1], halo_send.at[0], halo_recv.at[0, 1], near[0][0]).wait_send()
 
     @pl.when(has_below)
     def _():
-        for f in range(frames):
-            down_copy(f).wait_send()
+        edge = features.at[:, rows - 1]
+        remote(edge, halo.at[:, 0], halo_send.at[1], halo_recv.at[0, 0], near[1][0]).wait_send()
 
     @pl.when(has_before)
     def _():
-        next_copy.wait_send()
-        for r in range(rows):
-            mix_copy(0, r).wait_send()
+        back.wait_send()
+
+    def all_of(frame, count, send, recv):
+        several = gathered.at[frame, 0:count]
+        return remote(several, several, send.at[0], recv.at[0], other_core)
 
     @pl.when(has_after)
     def _():
-        for r in range(rows):
-            mix_copy(1, r).wait_send()
-        for copy in ahead_sends:
-            copy.wait_send()
-
-    @pl.when(is_first)
-    def _():
-        for copy in zero_sends:
-            copy.wait_send()
+        onward.wait_send()
+        all_of(0, n_rows, ahead_send, ahead_recv).wait_send()
+
+    if n_rows > 1:
+
+        @pl.when(is_first)
+        def _():
+            all_of(0, n_rows - 1, zero_send, ahead_recv).wait_send()
 
     widen.wait()
     fold_out[...] = fold[...]
-    for copy in sends:
-        copy.wait()
+    if n_rows > 1:
+        all_of(1, n_rows - 1, all_send, all_recv).wait()
+
+        @pl.when(is_first)
+        def _():
+            all_of(0, n_rows - 1, zero_send, ahead_recv).wait_recv()
 
     @pl.when(has_before)
     def _():
-        ahead_sends[0].wait_recv()
-
-    for copy in ahead_sends[1:]:
-        copy.wait_recv()
+        all_of(0, n_rows, ahead_send, ahead_recv).wait_recv()
+
     block_out[...] = gathered[...]
 
 
@@ -559,7 +575,7 @@
         in_specs=[hbm] * 9,
         out_specs=(vmem, vmem, vmem, vmem),
         scratch_shapes=[
-            pltpu.VMEM((frames + 1, rows, columns, channels), BF16),
+            pltpu.VMEM(features.shape, BF16),
             pltpu.VMEM((frames, 2, columns, channels), BF16),
             pltpu.VMEM((frames, columns, (rows + 2) * 3 * channels), BF16),
             pltpu.VMEM((9 * channels, channels), BF16),
@@ -574,6 +590,7 @@
             pltpu.VMEM((depth, width), BF16),
             pltpu.VMEM((frames, rows * columns, channels), BF16),
             pltpu.VMEM((frames, rows * columns, channels), BF16),
+            pltpu.VMEM((rows * columns, channels), BF16),
             pltpu.VMEM((frames, rows * columns, channels), F32),
             pltpu.VMEM((columns, LANES), F32),
             pltpu.VMEM((tokens, LANES), BF16),
@@ -588,14 +605,12 @@
             pltpu.VMEM((quads + later, 1, width), F32),
             pltpu.VMEM((frames, n_rows, tokens, LANES), BF16),
             pltpu.VMEM((PATCH, channels, LANES), BF16),
-            dma((10,)),
-            dma((frames, 2)), dma((frames, 2)),
-            dma((1,)), dma((1,)),
-            dma((frames, rows)), dma((frames, rows)),
-            dma((n_rows,)), dma((n_rows,)),
-            dma((n_rows,)), dma((n_rows,)), dma((n_rows,)),
-            dma((2 * quads + later + 1,)), dma((2 * quads + later + 1,)),
-            dma((quads + later,)), dma((quads + later,)),
+            dma((9 if aligned else 10,)),
+            dma((2,)), dma((frames, 2)),
+            dma((2,)), dma((2,)),
+            dma((1,)), dma((1,)), dma((1,)), dma((1,)), dma((1,)),
+            dma((4 + later,)), dma((4 + later,)),
+            dma((2 + later,)), dma((2 + later,)),
             pltpu.SemaphoreType.REGULAR((max(n_rows - 1, 1),)),
             pltpu.SemaphoreType.REGULAR((1,)),
         ],

time: 21.2 us -> 20.1 us (0.948)
  the two profiles are of different devices: /device:TPU:6 before, /device:TPU:0 now
where the time goes in v5:
time: 20.1 us; the launch traced here: 20 us
  Pallas kernels  20 us (100%)
    pallas_call x1, Pallas kernels, per_device(): pl.pallas_call(functools.partial(encode, n_tm, n_rows, split, aligned), o...  17.8 us
    pallas_call x1, Pallas kernels, per_device(): pl.pallas_call(project, out_shape=jax.ShapeDtypeStruct((count, width), F3...  2.16 us

profile of v5, /device:TPU:0, one launch (start us, length us, event | category | flops | bytes accessed | tf_op | source)
XLA Modules:
  0.0 20.0 jit_solution(15798557830437705465)
XLA Ops:
  0.0 17.8 %encode.1 = (bf16[2,4,48,128]{3,2,1,0:T(8,128)(2,1)S(1)}, bf16[2,4,8,2304]{3,2,1,0:T(8,128)(2,1)S(1)}, f32[1,2304]{1,0:T(1,128)S(1)}, bf16[3,64,64]{2,1,0:T(8,128)(2,1)S(1)}) custom-call(bf16[2,2,96,512]{3,2,1,0:T(8,128)(2,1)} %features.1, bf16[4608,512]{1,0:T(8,128)(2,1)} %bitcast.6, bf16[3,512,512]{2,1,0:T(8,128)(2,1)} %temporal_hbm.1, ...), custom_call_target="tpu_custom_call" | custom-call | tf_op jit(solution)/shard_map/encode/pallas_call | solution.py:567
  17.8 2.2 %project.1 = f32[384,2304]{1,0:T(8,128)} custom-call(bf16[2,4,48,128]{3,2,1,0:T(8,128)(2,1)S(1)} %get-tuple-element.9.block, bf16[64,2304]{1,0:T(8,128)(2,1)S(1)} %bitcast.5, f32[1,2304]{1,0:T(1,128)S(1)} %get-tuple-element.11.shift, bf16[3,64,64]{2,1,0:T(8,128)(2,1)S(1)} %get-tuple-element.12.gram), custom_call_target="tpu_custom_call" | custom-call | tf_op jit(solution)/shard_map/project/pallas_call | solution.py:633

commit v6 on v5

--- a/solution.py
+++ b/solution.py
@@ -126,7 +126,8 @@
 
     order = (core, 1 - core)
     pl.semaphore_wait(barrier, len(partners) + count_rows + count_tiles)
-    for f in order:
+
+    def send_rows(f):
         @pl.when(has_above)
         def _():
             up_copy(f).start()
@@ -134,6 +135,8 @@
         @pl.when(has_below)
         def _():
             down_copy(f).start()
+
+    send_rows(order[0])
 
     phases = n_rows - 1
     done_phases = [0]
@@ -228,6 +231,7 @@
     ]
     for copy in core_copies:
         copy.start()
+    send_rows(order[1])
 
     inner = taps[:, :, span : 3 * span].reshape(frames * columns, 2 * span)
     direct_copies = []
@@ -351,26 +355,24 @@
     def _():
         place_heads()
 
+    early = 2 * row < n_rows
+    soon = jnp.logical_and(early, lax.rem(tile // 2, 2) == 1)
     finish_frame(order[0])
     next_phase()
+
+    @pl.when(soon)
+    def _():
+        end_direct()
+
     finish_frame(order[1])
 
     @pl.when(core == 1)
     def _():
         place_heads()
 
-    own_frames = jnp.concatenate([mixed[0], mixed[1]], axis=1)
-    partial[0] = dot(own_frames, temp_w[0:2].reshape(2 * channels, channels))
-    partial[1] = dot(own_frames, temp_w[1:3].reshape(2 * channels, channels))
-
-    early = 2 * row < n_rows
-
-    @pl.when(early)
+    @pl.when(jnp.logical_and(early, jnp.logical_not(soon)))
     def _():
         end_direct()
-
-    while done_phases[0] < phases:
-        next_phase()
 
     tokens = columns // PATCH
     out_lane = lax.broadcasted_iota(jnp.int32, (tokens, LANES), 1)
@@ -407,10 +409,29 @@
     ]
 
     is_first = tile == 0
+    last_first = jnp.logical_or(is_first, core == 1)
+
+    def of_own(tap):
+        own_frames = jnp.concatenate([mixed[0], mixed[1]], axis=1)
+        return dot(own_frames, temp_w[tap : tap + 2].reshape(2 * channels, channels))
+
+    @pl.when(last_first)
+    def _():
+        partial[1] = of_own(1)
+
+    @pl.when(jnp.logical_not(last_first))
+    def _():
+        partial[0] = of_own(0)
 
     @pl.when(is_first)
     def _():
         gathered[0, row] = patches_of(bracket[...].astype(F32))
+
+    while done_phases[0] < phases:
+        next_phase()
+
+    @pl.when(is_first)
+    def _():
         for copy in zero_sends:
             copy.start()
 
@@ -424,7 +445,6 @@
         for copy in sends:
             copy.start()
 
-    last_first = jnp.logical_or(is_first, core == 1)
     late = jnp.logical_not(early)
 
     @pl.when(last_first)
@@ -437,6 +457,10 @@
 
     @pl.when(has_after)
     def _():
+        @pl.when(last_first)
+        def _():
+            partial[0] = of_own(0)
+
         back.wait_recv()
         ahead[...] = patches_of(partial[0] + side[1].astype(F32))
         for copy in ahead_sends:
@@ -448,6 +472,7 @@
 
     @pl.when(jnp.logical_not(last_first))
     def _():
+        partial[1] = of_own(1)
         last_frame()
 
     if direct:

time: 20.1 us -> 19.6 us (0.975)
  Pallas kernels: 20 us -> 19.5 us
    pallas_call x1, Pallas kernels: 17.8 us -> 17.3 us  [per_device(): pl.pallas_call(functools.partial(encode, n_tm, n_rows, split, aligned), o...]
where the time goes in v6:
time: 19.6 us; the launch traced here: 19.5 us
  Pallas kernels  19.5 us (99%)
    pallas_call x1, Pallas kernels, per_device(): pl.pallas_call(functools.partial(encode, n_tm, n_rows, split, aligned), o...  17.3 us
    pallas_call x1, Pallas kernels, per_device(): pl.pallas_call(project, out_shape=jax.ShapeDtypeStruct((count, width), F3...  2.16 us

profile of v6, /device:TPU:0, one launch (start us, length us, event | category | flops | bytes accessed | tf_op | source)
XLA Modules:
  0.0 19.5 jit_solution(3538655092640329536)
XLA Ops:
  0.0 17.3 %encode.1 = (bf16[2,4,48,128]{3,2,1,0:T(8,128)(2,1)S(1)}, bf16[2,4,8,2304]{3,2,1,0:T(8,128)(2,1)S(1)}, f32[1,2304]{1,0:T(1,128)S(1)}, bf16[3,64,64]{2,1,0:T(8,128)(2,1)S(1)}) custom-call(bf16[2,2,96,512]{3,2,1,0:T(8,128)(2,1)} %features.1, bf16[4608,512]{1,0:T(8,128)(2,1)} %bitcast.6, bf16[3,512,512]{2,1,0:T(8,128)(2,1)} %temporal_hbm.1, ...), custom_call_target="tpu_custom_call" | custom-call | tf_op jit(solution)/shard_map/encode/pallas_call | solution.py:592
  17.3 2.2 %project.1 = f32[384,2304]{1,0:T(8,128)} custom-call(bf16[2,4,48,128]{3,2,1,0:T(8,128)(2,1)S(1)} %get-tuple-element.9.block, bf16[64,2304]{1,0:T(8,128)(2,1)S(1)} %bitcast.5, f32[1,2304]{1,0:T(1,128)S(1)} %get-tuple-element.11.shift, bf16[3,64,64]{2,1,0:T(8,128)(2,1)S(1)} %get-tuple-element.12.gram), custom_call_target="tpu_custom_call" | custom-call | tf_op jit(solution)/shard_map/project/pallas_call | solution.py:658

commit v7 on v6

--- a/solution.py
+++ b/solution.py
@@ -357,23 +357,7 @@
 
     early = 2 * row < n_rows
     soon = jnp.logical_and(early, lax.rem(tile // 2, 2) == 1)
-    finish_frame(order[0])
-    next_phase()
-
-    @pl.when(soon)
-    def _():
-        end_direct()
-
-    finish_frame(order[1])
-
-    @pl.when(core == 1)
-    def _():
-        place_heads()
-
-    @pl.when(jnp.logical_and(early, jnp.logical_not(soon)))
-    def _():
-        end_direct()
-
+    is_first = tile == 0
     tokens = columns // PATCH
     out_lane = lax.broadcasted_iota(jnp.int32, (tokens, LANES), 1)
     even_lane = lax.rem(out_lane // latent, PATCH) == 0
@@ -384,6 +368,28 @@
         even = lat[pl.ds(0, tokens, stride=PATCH), :]
         odd = lat[pl.ds(1, tokens, stride=PATCH), :]
         return jnp.where(even_lane, even, odd).astype(BF16)
+
+    finish_frame(order[0])
+
+    @pl.when(is_first)
+    def _():
+        gathered[0, row] = patches_of(bracket[...].astype(F32))
+
+    next_phase()
+
+    @pl.when(soon)
+    def _():
+        end_direct()
+
+    finish_frame(order[1])
+
+    @pl.when(core == 1)
+    def _():
+        place_heads()
+
+    @pl.when(jnp.logical_and(early, jnp.logical_not(soon)))
+    def _():
+        end_direct()
 
     def away(d):
         return lax.rem(row + d, n_rows)
@@ -408,7 +414,6 @@
         for d in range(1, n_rows)
     ]
 
-    is_first = tile == 0
     last_first = jnp.logical_or(is_first, core == 1)
 
     def of_own(tap):
@@ -422,10 +427,6 @@
     @pl.when(jnp.logical_not(last_first))
     def _():
         partial[0] = of_own(0)
-
-    @pl.when(is_first)
-    def _():
-        gathered[0, row] = patches_of(bracket[...].astype(F32))
 
     while done_phases[0] < phases:
         next_phase()
@@ -544,18 +545,18 @@
 def project(block, fold, shift, gram, out, held, sems):
     pdim, width = fold.shape
     frames, n_rows, tokens, _ = block.shape
-    parts = 4
-    lines = n_rows * tokens // parts
+    total = n_rows * tokens
+    cuts = [0, 16, 48, 96] + list(range(144, total, 48)) + [total]
     copies = []
     for f in range(frames):
-        patches = block[f].reshape(n_rows * tokens, LANES)[:, :pdim]
-        for n in range(parts):
-            own = patches[n * lines : (n + 1) * lines]
+        patches = block[f].reshape(total, LANES)[:, :pdim]
+        for n, (low, high) in enumerate(zip(cuts, cuts[1:])):
+            own = patches[low:high]
             moved = dot(own, gram[0]) + dot(own, gram[1]) + dot(own, gram[2])
             spread = jnp.maximum(jnp.sum(moved * own.astype(F32), axis=-1, keepdims=True), 0.0)
-            here = pl.ds((f * parts + n) * lines, lines)
+            here = pl.ds(f * total + low, high - low)
             held[here] = dot(own, fold[...]) * lax.rsqrt(spread + EPS) + shift[...]
-            copy = pltpu.make_async_copy(held.at[here], out.at[here], sems.at[f * parts + n])
+            copy = pltpu.make_async_copy(held.at[here], out.at[here], sems.at[len(copies)])
             copy.start()
             copies.append(copy)
     for copy in copies:
@@ -660,7 +661,7 @@
         out_shape=jax.ShapeDtypeStruct((count, width), F32),
         in_specs=[vmem] * 4,
         out_specs=hbm,
-        scratch_shapes=[pltpu.VMEM((count, width), F32), dma((4 * frames,))],
+        scratch_shapes=[pltpu.VMEM((count, width), F32), dma((count // 48 + 4 * frames,))],
         compiler_params=pltpu.CompilerParams(vmem_limit_bytes=32 * 2**20),
         name="project",
     )(block, fold.reshape(pdim, width), shift_row, gram)

time: 19.6 us -> 19.7 us (level)
  no operation moved by 1% of the time
where the time goes in v7:
time: 19.7 us; the launch traced here: 19.5 us
  Pallas kernels  19.5 us (99%)
    pallas_call x1, Pallas kernels, per_device(): pl.pallas_call(functools.partial(encode, n_tm, n_rows, split, aligned), o...  17.3 us
    pallas_call x1, Pallas kernels, per_device(): pl.pallas_call(project, out_shape=jax.ShapeDtypeStruct((count, width), F3...  2.19 us

profile of v7, /device:TPU:0, one launch (start us, length us, event | category | flops | bytes accessed | tf_op | source)
XLA Modules:
  0.0 19.5 jit_solution(15649488100790163142)
XLA Ops:
  0.0 17.3 %encode.1 = (bf16[2,4,48,128]{3,2,1,0:T(8,128)(2,1)S(1)}, bf16[2,4,8,2304]{3,2,1,0:T(8,128)(2,1)S(1)}, f32[1,2304]{1,0:T(1,128)S(1)}, bf16[3,64,64]{2,1,0:T(8,128)(2,1)S(1)}) custom-call(bf16[2,2,96,512]{3,2,1,0:T(8,128)(2,1)} %features.1, bf16[4608,512]{1,0:T(8,128)(2,1)} %bitcast.6, bf16[3,512,512]{2,1,0:T(8,128)(2,1)} %temporal_hbm.1, ...), custom_call_target="tpu_custom_call" | custom-call | tf_op jit(solution)/shard_map/encode/pallas_call | solution.py:593
  17.3 2.2 %project.1 = f32[384,2304]{1,0:T(8,128)} custom-call(bf16[2,4,48,128]{3,2,1,0:T(8,128)(2,1)S(1)} %get-tuple-element.9.block, bf16[64,2304]{1,0:T(8,128)(2,1)S(1)} %bitcast.5, f32[1,2304]{1,0:T(1,128)S(1)} %get-tuple-element.11.shift, bf16[3,64,64]{2,1,0:T(8,128)(2,1)S(1)} %get-tuple-element.12.gram), custom_call_target="tpu_custom_call" | custom-call | tf_op jit(solution)/shard_map/project/pallas_call | solution.py:659
